TPU v7x, 32 devices: a whole 2x2x4 slice. The times are simulated.
32 devices in a mesh: trial: 4 (over z), lat: 2 (over x), lon: 2 (over core), lev: 2 (over y).
Axes of the slice: x: 2, y: 2, z: 4, core: 2. Of those that a mesh axis runs over, the one named last changes fastest.
Arguments:
- density: float32 [32, 32, 256, 128], P(('trial', 'lat'), 'lon', 'lev'), parts along dimension 0, may hold values from 0.5 to 2
- crowding: float32 [32, 32, 256, 128], P(('trial', 'lat'), 'lon', 'lev'), parts along dimension 0, may hold values from 0.5 to 2
Outputs:
- scaled_field: float32 [32, 32, 256, 128], P(('trial', 'lat'), 'lon', 'lev'), parts along dimension 0
- density_end: float32 [32, 32, 256, 128], P(('trial', 'lat'), 'lon', 'lev'), parts along dimension 0
There are 4 independent parts, one for each index of `trial`. A program takes and returns all parts, laid end to end along the dimension named above; each array names one. Nothing has to cross between parts.
All inputs are finite; a program needn't handle non-finite values.
Results may differ from a plain program's by a relative error of at most 0.000058.
Values sent between devices are 32-bit elements; how exact they have to be, the bound alone decides.
A program may use at most 64 MiB of HBM per device.

v0:
```python
import functools

import jax
import jax.numpy as jnp
from jax import lax
from jax.experimental import pallas as pl
from jax.experimental.pallas import tpu as pltpu
from jax.sharding import PartitionSpec as P

STEPS = 4
PAD = 8
MESH = pl.DeviceIdType.MESH


def with_halo(cells, sides, width):
    for axis, dim in sides:
        count = lax.axis_size(axis)
        ends = count - 1
        head = lax.slice_in_dim(cells, 0, width, axis=dim)
        tail = lax.slice_in_dim(cells, cells.shape[dim] - width, cells.shape[dim], axis=dim)
        cells = jnp.concatenate(
            [
                lax.ppermute(tail, axis, [(i, (i + 1) % count) for i in range(ends)]),
                cells,
                lax.ppermute(head, axis, [((i + 1) % count, i) for i in range(ends)]),
            ],
            axis=dim,
        )
    return cells


def inner_cells(values, dims):
    for dim in dims:
        values = lax.slice_in_dim(values, 1, values.shape[dim] - 1, axis=dim)
    return values


def side_cells(values, dim, start, dims):
    others = [other for other in dims if other != dim]
    values = inner_cells(values, others)
    return lax.slice_in_dim(values, start, start + values.shape[dim] - 2, axis=dim)


def advance(padded, crowding):
    middle = inner_cells(padded, (0, 1, 2))
    lower = [side_cells(padded, dim, 0, (0, 1, 2)) for dim in (0, 1, 2)]
    upper = [side_cells(padded, dim, 2, (0, 1, 2)) for dim in (0, 1, 2)]
    spread = lower[0] + upper[0] + lower[1] + upper[1] + lower[2] + upper[2] - 6.0 * middle
    return middle + 0.1 * spread + 0.2 * middle * (1.0 - middle * crowding)


def general(density, crowding):
    for step in range(STEPS):
        padded = with_halo(density, (("lat", 0), ("lon", 1), ("lev", 2)), 1)
        density = advance(padded, crowding)
    count = density.shape[1] * lax.axis_size("lon")
    moved = density - 1.0
    totals, squares = lax.psum(
        (jnp.sum(moved, axis=1, keepdims=True), jnp.sum(moved * moved, axis=1, keepdims=True)),
        "lon",
    )
    line_mean = 1.0 + totals / count
    centred = density - line_mean
    line_variance = squares / count - totals / count * (totals / count)
    return (centred * lax.rsqrt(line_variance + 0.0001), density)


def tree_sum(terms):
    terms = list(terms)
    while len(terms) > 1:
        terms = [sum(terms[i : i + 2][1:], terms[i]) for i in range(0, len(terms), 2)]
    return terms[0]


def kernel(lons, levs, coarse, fine, dens, crowd, out_scaled, out_dens,
           field, cap, stats, peers, load_sem, edge_sem, face_send, face_recv,
           lon_send, lon_recv, lev_send, lev_recv, stat_send, stat_recv):
    rows, cols, deep, lanes = dens.shape
    spans, parts = fine, len(fine)
    lat, lon, lev = lax.axis_index("lat"), lax.axis_index("lon"), lax.axis_index("lev")
    has_left, has_right = lon > 0, lon < lons - 1
    has_down, has_up = lev > 0, lev < levs - 1

    def place(r):
        return (1 - lat) * (rows - r) + lat * (r - 1)

    first = [
        pltpu.make_async_copy(
            dens.at[place(1), :, pl.ds(at, span)],
            field.at[0, 1, pl.ds(1, cols), pl.ds(PAD + at, span)],
            edge_sem.at[k])
        for k, (at, span) in enumerate(coarse)
    ]
    loads = []
    for r in range(1, rows + 1):
        if r > 1:
            loads.append(pltpu.make_async_copy(
                dens.at[place(r)],
                field.at[0, r, pl.ds(1, cols), pl.ds(PAD, deep)],
                load_sem.at[0, r - 1]))
        loads.append(pltpu.make_async_copy(
            crowd.at[place(r)], cap.at[r - 1], load_sem.at[1, r - 1]))
    for copy in first + loads:
        copy.start()

    barrier = pltpu.get_barrier_semaphore()
    pl.semaphore_signal(barrier, inc=1, device_id={"lat": 1 - lat}, device_id_type=MESH)
    for j in range(1, lons):
        pl.semaphore_signal(barrier, inc=1, device_id={"lon": lax.rem(lon + j, lons)}, device_id_type=MESH)
    if levs > 1:
        @pl.when(has_down)
        def _():
            pl.semaphore_signal(barrier, inc=1, device_id={"lev": lev - 1}, device_id_type=MESH)

        @pl.when(has_up)
        def _():
            pl.semaphore_signal(barrier, inc=1, device_id={"lev": lev + 1}, device_id_type=MESH)
    pl.semaphore_wait(barrier, lons + has_down.astype(jnp.int32) + has_up.astype(jnp.int32))

    def chunks(t):
        return fine if t == STEPS - 1 else coarse

    def face(t, k):
        at, span = chunks(t)[k]
        return pltpu.make_async_remote_copy(
            src_ref=field.at[t, 1, pl.ds(1, cols), pl.ds(PAD + at, span)],
            dst_ref=field.at[t, 0, pl.ds(1, cols), pl.ds(PAD + at, span)],
            send_sem=face_send.at[t, k],
            recv_sem=face_recv.at[t, k],
            device_id={"lat": 1 - lat},
            device_id_type=MESH,
        )

    def lon_side(t, right):
        own, theirs = (cols, 0) if right else (1, cols + 1)
        span = pl.ds(1, rows)
        return pltpu.make_async_remote_copy(
            src_ref=field.at[t, span, own, pl.ds(PAD, deep)],
            dst_ref=field.at[t, span, theirs, pl.ds(PAD, deep)],
            send_sem=lon_send.at[t, int(right)],
            recv_sem=lon_recv.at[t, int(right)],
            device_id={"lon": lon + 1 if right else lon - 1},
            device_id_type=MESH,
        )

    def lev_side(t, up):
        own, theirs = (PAD + deep - 1, PAD - 1) if up else (PAD, PAD + deep)
        span = (pl.ds(1, rows), pl.ds(1, cols))
        return pltpu.make_async_remote_copy(
            src_ref=field.at[t, span[0], span[1], pl.ds(own, 1)],
            dst_ref=field.at[t, span[0], span[1], pl.ds(theirs, 1)],
            send_sem=lev_send.at[t, int(up)],
            recv_sem=lev_recv.at[t, int(up)],
            device_id={"lev": lev + 1 if up else lev - 1},
            device_id_type=MESH,
        )

    def sides(t, act):
        if lons > 1:
            pl.when(has_right)(lambda: act(lon_side(t, True), 1))
            pl.when(has_left)(lambda: act(lon_side(t, False), 0))
        if levs > 1:
            pl.when(has_up)(lambda: act(lev_side(t, True), 1))
            pl.when(has_down)(lambda: act(lev_side(t, False), 0))

    def start_sides(t):
        sides(t, lambda copy, _: copy.start())

    def wait_sides_sent(t):
        sides(t, lambda copy, _: copy.wait_send())

    def wait_sides(t):
        if lons > 1:
            pl.when(has_left)(lambda: lon_side(t, True).wait_recv())
            pl.when(has_right)(lambda: lon_side(t, False).wait_recv())
        if levs > 1:
            pl.when(has_down)(lambda: lev_side(t, True).wait_recv())
            pl.when(has_up)(lambda: lev_side(t, False).wait_recv())

    def stat(part, j):
        if part < parts:
            pick = (0, slice(None), pl.ds(*spans[part]))
        else:
            pick = (pl.ds(1, rows - 1),)
        return pltpu.make_async_remote_copy(
            src_ref=stats.at[pick],
            dst_ref=peers.at[(j - 1,) + pick],
            send_sem=stat_send.at[part, j - 1],
            recv_sem=stat_recv.at[part, j - 1],
            device_id={"lon": lax.rem(lon + j, lons)},
            device_id_type=MESH,
        )

    for k in range(len(coarse)):
        first[k].wait()
        face(0, k).start()

    def clear_cols(at):
        for t in range(STEPS):
            def row(i, _, t=t):
                field[t, i, at, pl.ds(PAD, deep)] = jnp.zeros((deep, lanes), jnp.float32)
                return 0
            lax.fori_loop(1, rows + 1, row, 0)

    def clear_level(at):
        for t in range(STEPS):
            def row(i, _, t=t):
                def col(c, _):
                    field[t, i, c, pl.ds(at, PAD)] = jnp.zeros((PAD, lanes), jnp.float32)
                    return 0
                return lax.fori_loop(1, cols + 1, col, 0)
            lax.fori_loop(1, rows + 1, row, 0)

    pl.when(jnp.logical_not(has_left))(lambda: clear_cols(0))
    pl.when(jnp.logical_not(has_right))(lambda: clear_cols(cols + 1))
    pl.when(jnp.logical_not(has_down))(lambda: clear_level(0))
    pl.when(jnp.logical_not(has_up))(lambda: clear_level(PAD + deep))

    for copy in loads:
        copy.wait()
    start_sides(0)

    def cell(t, r, c, at, span, last):
        here = field[t, r, c, pl.ds(PAD + at, span)]
        near = (field[t, r, c - 1, pl.ds(PAD + at, span)] + field[t, r, c + 1, pl.ds(PAD + at, span)])
        near += (field[t, r, c, pl.ds(PAD - 1 + at, span)] + field[t, r, c, pl.ds(PAD + 1 + at, span)])
        near += field[t, r - 1, c, pl.ds(PAD + at, span)]
        if not last:
            near += field[t, r + 1, c, pl.ds(PAD + at, span)]
        limit = cap[r - 1, c - 1, pl.ds(at, span)]
        return here * (0.6 - 0.2 * (here * limit)) + 0.1 * near

    def advance_row(t, r, at, span, last):
        def col(c, _):
            field[t + 1, r, c, pl.ds(PAD + at, span)] = cell(t, r, c, at, span, last)
            return 0
        lax.fori_loop(1, cols + 1, col, 0)

    for t in range(STEPS - 1):
        wait_sides(t)

        def inner(r, _, t=t):
            advance_row(t, r, 0, deep, False)
            return 0

        lax.fori_loop(2, rows, inner, 0)
        advance_row(t, rows, 0, deep, True)
        for k in range(len(coarse)):
            face(t, k).wait_recv()
            advance_row(t, 1, *coarse[k], False)
            for j, (at, _) in enumerate(chunks(t + 1)):
                if coarse[k][0] <= at < sum(coarse[k]):
                    face(t + 1, j).start()
        start_sides(t + 1)

    t = STEPS - 1
    wait_sides(t)

    def finish(r, at, last):
        values = [cell(t, r, c, at, 8, last) for c in range(1, cols + 1)]
        for c in range(cols):
            out_dens[place(r), c, pl.ds(at, 8)] = values[c]
        total = tree_sum(values)
        mean = total * (1.0 / cols)
        stats[r - 1, 0, pl.ds(at, 8)] = total
        stats[r - 1, 1, pl.ds(at, 8)] = tree_sum([(v - mean) * (v - mean) for v in values])

    def scale(r, at):
        pair = [(stats[r - 1, 0, pl.ds(at, 8)], stats[r - 1, 1, pl.ds(at, 8)])]
        for j in range(lons - 1):
            pair.append((peers[j, r - 1, 0, pl.ds(at, 8)], peers[j, r - 1, 1, pl.ds(at, 8)]))
        count = cols * lons
        mean = tree_sum([p[0] for p in pair]) * (1.0 / count)
        square = tree_sum([p[1] + cols * (p[0] * (1.0 / cols) - mean) ** 2 for p in pair])
        gain = lax.rsqrt(square * (1.0 / count) + 0.0001)
        for c in range(cols):
            out_scaled[place(r), c, pl.ds(at, 8)] = (out_dens[place(r), c, pl.ds(at, 8)] - mean) * gain

    def tiles(first, many, act):
        def tile(i, _):
            act(pl.multiple_of(i * 8, 8))
            return 0
        lax.fori_loop(first // 8, (first + many) // 8, tile, 0)

    def each_inner(act):
        def row(r, _):
            tiles(0, deep, lambda at: act(r, at))
            return 0
        lax.fori_loop(2, rows, row, 0)

    each_inner(lambda r, at: finish(r, at, False))
    tiles(0, deep, lambda at: finish(rows, at, True))
    for j in range(1, lons):
        stat(parts, j).start()
    for k in range(parts):
        face(t, k).wait_recv()
        tiles(*spans[k], lambda at: finish(1, at, False))
        for j in range(1, lons):
            stat(k, j).start()
        if k == 0:
            for j in range(1, lons):
                stat(parts, j).wait_recv()
            each_inner(scale)
            tiles(0, deep, lambda at: scale(rows, at))
        else:
            for j in range(1, lons):
                stat(k - 1, j).wait_recv()
            tiles(*spans[k - 1], lambda at: scale(1, at))
    for s in range(STEPS):
        for k in range(len(chunks(s))):
            face(s, k).wait_send()
        wait_sides_sent(s)
    for j in range(1, lons):
        stat(parts - 1, j).wait_recv()
    tiles(*spans[parts - 1], lambda at: scale(1, at))
    for j in range(1, lons):
        for part in range(parts + 1):
            stat(part, j).wait_send()


def writer(scaled, dens, out_scaled, out_dens, sems):
    copies = []
    for i, (src, dst) in enumerate(((scaled, out_scaled), (dens, out_dens))):
        for r in range(src.shape[0]):
            copies.append(pltpu.make_async_copy(src.at[r], dst.at[r], sems.at[i, r]))
    for copy in copies:
        copy.start()
    for copy in copies:
        copy.wait()


def written(scaled, dens):
    out = jax.ShapeDtypeStruct(dens.shape, dens.dtype)
    return pl.pallas_call(
        writer,
        out_shape=(out, out),
        in_specs=[pl.BlockSpec(memory_space=pltpu.VMEM)] * 2,
        out_specs=[pl.BlockSpec(memory_space=pl.ANY)] * 2,
        scratch_shapes=[pltpu.SemaphoreType.DMA((2, dens.shape[0]))],
        compiler_params=pltpu.CompilerParams(vmem_limit_bytes=2**20),
    )(
        pltpu.with_memory_space_constraint(scaled, pltpu.VMEM),
        pltpu.with_memory_space_constraint(dens, pltpu.VMEM),
    )


def one_kernel(lons, levs, density, crowding):
    rows, cols, deep, lanes = density.shape
    half = deep // 2
    coarse = [(0, half), (half, half)]
    fine = coarse[:1] + [(half, half - 8), (deep - 8, 8)]
    parts = len(fine)
    sem = pltpu.SemaphoreType.DMA
    peers = max(lons - 1, 1)
    out = pltpu.VMEM(density.shape, jnp.float32)
    return pl.pallas_call(
        functools.partial(kernel, lons, levs, coarse, fine),
        out_shape=(out, out),
        in_specs=[pl.BlockSpec(memory_space=pl.ANY)] * 2,
        out_specs=[pl.BlockSpec(memory_space=pltpu.VMEM)] * 2,
        scratch_shapes=[
            pltpu.VMEM((STEPS, rows + 1, cols + 2, deep + 2 * PAD, lanes), jnp.float32),
            pltpu.VMEM((rows, cols, deep, lanes), jnp.float32),
            pltpu.VMEM((rows, 2, deep, lanes), jnp.float32),
            pltpu.VMEM((peers, rows, 2, deep, lanes), jnp.float32),
            sem((2, rows)),
            sem((len(coarse),)),
            sem((STEPS, parts)),
            sem((STEPS, parts)),
            sem((STEPS, 2)),
            sem((STEPS, 2)),
            sem((STEPS, 2)),
            sem((STEPS, 2)),
            sem((parts + 1, peers)),
            sem((parts + 1, peers)),
        ],
        compiler_params=pltpu.CompilerParams(
            collective_id=0, has_side_effects=True, vmem_limit_bytes=VMEM_LIMIT
        ),
    )(density, crowding)


VMEM_LIMIT = 44 * 2**20


def solution(mesh):
    lats, lons, levs = mesh.shape["lat"], mesh.shape["lon"], mesh.shape["lev"]

    def shards(density, crowding):
        rows, cols, deep, lanes = density.shape
        words = lanes * (
            STEPS * (rows + 1) * (cols + 2) * (deep + 2 * PAD)
            + 3 * rows * cols * deep
            + 2 * lons * rows * deep
        )
        fits = lats == 2 and rows > 1 and lanes == 128 and deep % 32 == 0 and 4 * words < VMEM_LIMIT
        if fits:
            return tuple(written(*one_kernel(lons, levs, density, crowding)))
        return general(density, crowding)

    spec = P(("trial", "lat"), "lon", "lev", None)
    return jax.shard_map(
        shards, mesh=mesh, in_specs=(spec, spec), out_specs=(spec, spec), check_vma=False
    )
```

profile of v0, /device:TPU:1, one launch (start us, length us, event | category | flops | bytes accessed | tf_op | source)
XLA Modules:
  0.0 100.3 jit_solution(10488187816553688914)
XLA Ops:
  0.6 96.3 %shard_map.41 = (f32[4,16,128,128]{3,2,1,0:T(8,128)S(1)}, f32[4,16,128,128]{3,2,1,0:T(8,128)S(1)}) custom-call(f32[4,16,128,128]{3,2,1,0:T(8,128)} %dens.1, f32[4,16,128,128]{3,2,1,0:T(8,128)} %crowd.1), custom_call_target="tpu_custom_call" | custom-call | tf_op jit(solution)/shard_map/pallas_call | solution.py:356
  96.9 3.4 %shard_map.42 = (f32[4,16,128,128]{3,2,1,0:T(8,128)}, f32[4,16,128,128]{3,2,1,0:T(8,128)}) custom-call(f32[4,16,128,128]{3,2,1,0:T(8,128)S(1)} %get-tuple-element.4.scaled, f32[4,16,128,128]{3,2,1,0:T(8,128)S(1)} %get-tuple-element.5.dens), custom_call_target="tpu_custom_call" | custom-call | tf_op jit(solution)/shard_map/pallas_call | solution.py:334
where the time goes:
time: 101 us; the launch traced here: 100 us
  Pallas kernels  99.6 us (99%)
    pallas_call x1, Pallas kernels, one_kernel(): pl.pallas_call(functools.partial(kernel, lons, levs, coarse, fine), out_s...  96.3 us
    pallas_call x1, Pallas kernels, written(): pl.pallas_call(writer, out_shape=(out, out), in_specs=[pl.BlockSpec(memor...  3.37 us

commit v1 on v0

--- a/solution.py
+++ b/solution.py
@@ -72,21 +72,56 @@
     return terms[0]
 
 
-def kernel(lons, levs, coarse, fine, dens, crowd, out_scaled, out_dens,
+def signal(sem, where):
+    pl.semaphore_signal(sem, inc=1, device_id=where, device_id_type=MESH)
+
+
+def split(deep):
+    half, first = deep // 2, max(8, deep // 32 * 8)
+    coarse = [(0, half), (half, half)]
+    fine = [(0, first), (first, half - first), (half, half - 8), (deep - 8, 8)]
+    return coarse, fine
+
+
+def place(r, rows):
+    lat = lax.axis_index("lat")
+    return (1 - lat) * (rows - r) + lat * (r - 1)
+
+
+def tiles(first, many, act):
+    def tile(i, _):
+        act(pl.multiple_of(i * 8, 8))
+        return 0
+    lax.fori_loop(first // 8, (first + many) // 8, tile, 0)
+
+
+def line_sums(values):
+    cols = len(values)
+    total = tree_sum(values)
+    mean = total * (1.0 / cols)
+    return total, tree_sum([(v - mean) * (v - mean) for v in values])
+
+
+def line_scale(pair, cols):
+    count = cols * len(pair)
+    mean = tree_sum([p[0] for p in pair]) * (1.0 / count)
+    square = tree_sum([p[1] + cols * (p[0] * (1.0 / cols) - mean) ** 2 for p in pair])
+    return mean, lax.rsqrt(square * (1.0 / count) + 0.0001)
+
+
+def kernel(lons, levs, dens, crowd, out_scaled, out_dens, edge, front,
            field, cap, stats, peers, load_sem, edge_sem, face_send, face_recv,
            lon_send, lon_recv, lev_send, lev_recv, stat_send, stat_recv):
     rows, cols, deep, lanes = dens.shape
-    spans, parts = fine, len(fine)
+    coarse, fine = split(deep)
     lat, lon, lev = lax.axis_index("lat"), lax.axis_index("lon"), lax.axis_index("lev")
     has_left, has_right = lon > 0, lon < lons - 1
     has_down, has_up = lev > 0, lev < levs - 1
-
-    def place(r):
-        return (1 - lat) * (rows - r) + lat * (r - 1)
+    late = lax.rem(lon, 2) == 1
 
     first = [
         pltpu.make_async_copy(
-            dens.at[place(1), :, pl.ds(at, span)],
+            dens.at[place(1, rows), :, pl.ds(at, span)],
             field.at[0, 1, pl.ds(1, cols), pl.ds(PAD + at, span)],
             edge_sem.at[k])
         for k, (at, span) in enumerate(coarse)
@@ -95,26 +130,21 @@
     for r in range(1, rows + 1):
         if r > 1:
             loads.append(pltpu.make_async_copy(
-                dens.at[place(r)],
+                dens.at[place(r, rows)],
                 field.at[0, r, pl.ds(1, cols), pl.ds(PAD, deep)],
                 load_sem.at[0, r - 1]))
         loads.append(pltpu.make_async_copy(
-            crowd.at[place(r)], cap.at[r - 1], load_sem.at[1, r - 1]))
+            crowd.at[place(r, rows)], cap.at[r - 1], load_sem.at[1, r - 1]))
+
+    barrier = pltpu.get_barrier_semaphore()
+    signal(barrier, {"lat": 1 - lat})
+    for j in range(1, lons):
+        signal(barrier, {"lon": lax.rem(lon + j, lons)})
+    if levs > 1:
+        pl.when(has_down)(lambda: signal(barrier, {"lev": lev - 1}))
+        pl.when(has_up)(lambda: signal(barrier, {"lev": lev + 1}))
     for copy in first + loads:
         copy.start()
-
-    barrier = pltpu.get_barrier_semaphore()
-    pl.semaphore_signal(barrier, inc=1, device_id={"lat": 1 - lat}, device_id_type=MESH)
-    for j in range(1, lons):
-        pl.semaphore_signal(barrier, inc=1, device_id={"lon": lax.rem(lon + j, lons)}, device_id_type=MESH)
-    if levs > 1:
-        @pl.when(has_down)
-        def _():
-            pl.semaphore_signal(barrier, inc=1, device_id={"lev": lev - 1}, device_id_type=MESH)
-
-        @pl.when(has_up)
-        def _():
-            pl.semaphore_signal(barrier, inc=1, device_id={"lev": lev + 1}, device_id_type=MESH)
     pl.semaphore_wait(barrier, lons + has_down.astype(jnp.int32) + has_up.astype(jnp.int32))
 
     def chunks(t):
@@ -177,16 +207,12 @@
             pl.when(has_down)(lambda: lev_side(t, True).wait_recv())
             pl.when(has_up)(lambda: lev_side(t, False).wait_recv())
 
-    def stat(part, j):
-        if part < parts:
-            pick = (0, slice(None), pl.ds(*spans[part]))
-        else:
-            pick = (pl.ds(1, rows - 1),)
+    def stat(j):
         return pltpu.make_async_remote_copy(
-            src_ref=stats.at[pick],
-            dst_ref=peers.at[(j - 1,) + pick],
-            send_sem=stat_send.at[part, j - 1],
-            recv_sem=stat_recv.at[part, j - 1],
+            src_ref=stats,
+            dst_ref=peers.at[j - 1],
+            send_sem=stat_send.at[j - 1],
+            recv_sem=stat_recv.at[j - 1],
             device_id={"lon": lax.rem(lon + j, lons)},
             device_id_type=MESH,
         )
@@ -220,21 +246,33 @@
         copy.wait()
     start_sides(0)
 
-    def cell(t, r, c, at, span, last):
+    def cell(t, r, c, at, span, below, above):
         here = field[t, r, c, pl.ds(PAD + at, span)]
         near = (field[t, r, c - 1, pl.ds(PAD + at, span)] + field[t, r, c + 1, pl.ds(PAD + at, span)])
         near += (field[t, r, c, pl.ds(PAD - 1 + at, span)] + field[t, r, c, pl.ds(PAD + 1 + at, span)])
-        near += field[t, r - 1, c, pl.ds(PAD + at, span)]
-        if not last:
+        if below:
+            near += field[t, r - 1, c, pl.ds(PAD + at, span)]
+        if above:
             near += field[t, r + 1, c, pl.ds(PAD + at, span)]
         limit = cap[r - 1, c - 1, pl.ds(at, span)]
         return here * (0.6 - 0.2 * (here * limit)) + 0.1 * near
 
     def advance_row(t, r, at, span, last):
         def col(c, _):
-            field[t + 1, r, c, pl.ds(PAD + at, span)] = cell(t, r, c, at, span, last)
+            value = cell(t, r, c, at, span, True, not last)
+            field[t + 1, r, c, pl.ds(PAD + at, span)] = value
+            if t == STEPS - 2 and isinstance(r, int) and r == 1:
+                front[c - 1, pl.ds(at, span)] = value
             return 0
         lax.fori_loop(1, cols + 1, col, 0)
+
+    def start_face(t, k):
+        if t == STEPS - 1 and k == len(fine) - 1:
+            return
+        if t == STEPS - 1 and k > 0:
+            pl.when(late)(lambda: face(t, k).start())
+        else:
+            face(t, k).start()
 
     for t in range(STEPS - 1):
         wait_sides(t)
@@ -250,37 +288,27 @@
             advance_row(t, 1, *coarse[k], False)
             for j, (at, _) in enumerate(chunks(t + 1)):
                 if coarse[k][0] <= at < sum(coarse[k]):
-                    face(t + 1, j).start()
+                    start_face(t + 1, j)
         start_sides(t + 1)
 
     t = STEPS - 1
     wait_sides(t)
 
     def finish(r, at, last):
-        values = [cell(t, r, c, at, 8, last) for c in range(1, cols + 1)]
+        values = [cell(t, r, c, at, 8, True, not last) for c in range(1, cols + 1)]
         for c in range(cols):
-            out_dens[place(r), c, pl.ds(at, 8)] = values[c]
-        total = tree_sum(values)
-        mean = total * (1.0 / cols)
-        stats[r - 1, 0, pl.ds(at, 8)] = total
-        stats[r - 1, 1, pl.ds(at, 8)] = tree_sum([(v - mean) * (v - mean) for v in values])
+            out_dens[r - 2, c, pl.ds(at, 8)] = values[c]
+        total, square = line_sums(values)
+        stats[r - 2, 0, pl.ds(at, 8)] = total
+        stats[r - 2, 1, pl.ds(at, 8)] = square
 
     def scale(r, at):
-        pair = [(stats[r - 1, 0, pl.ds(at, 8)], stats[r - 1, 1, pl.ds(at, 8)])]
+        pair = [(stats[r - 2, 0, pl.ds(at, 8)], stats[r - 2, 1, pl.ds(at, 8)])]
         for j in range(lons - 1):
-            pair.append((peers[j, r - 1, 0, pl.ds(at, 8)], peers[j, r - 1, 1, pl.ds(at, 8)]))
-        count = cols * lons
-        mean = tree_sum([p[0] for p in pair]) * (1.0 / count)
-        square = tree_sum([p[1] + cols * (p[0] * (1.0 / cols) - mean) ** 2 for p in pair])
-        gain = lax.rsqrt(square * (1.0 / count) + 0.0001)
+            pair.append((peers[j, r - 2, 0, pl.ds(at, 8)], peers[j, r - 2, 1, pl.ds(at, 8)]))
+        mean, gain = line_scale(pair, cols)
         for c in range(cols):
-            out_scaled[place(r), c, pl.ds(at, 8)] = (out_dens[place(r), c, pl.ds(at, 8)] - mean) * gain
-
-    def tiles(first, many, act):
-        def tile(i, _):
-            act(pl.multiple_of(i * 8, 8))
-            return 0
-        lax.fori_loop(first // 8, (first + many) // 8, tile, 0)
+            out_scaled[r - 2, c, pl.ds(at, 8)] = (out_dens[r - 2, c, pl.ds(at, 8)] - mean) * gain
 
     def each_inner(act):
         def row(r, _):
@@ -291,93 +319,256 @@
     each_inner(lambda r, at: finish(r, at, False))
     tiles(0, deep, lambda at: finish(rows, at, True))
     for j in range(1, lons):
-        stat(parts, j).start()
-    for k in range(parts):
+        stat(j).start()
+
+    def base(c, _):
+        edge[c - 1] = cell(t, 1, c, 0, deep, False, True)
+        return 0
+
+    lax.fori_loop(1, cols + 1, base, 0)
+    for j in range(1, lons):
+        stat(j).wait_recv()
+    each_inner(scale)
+    tiles(0, deep, lambda at: scale(rows, at))
+
+    def add_face(k):
+        at, span = fine[k]
         face(t, k).wait_recv()
-        tiles(*spans[k], lambda at: finish(1, at, False))
-        for j in range(1, lons):
-            stat(k, j).start()
-        if k == 0:
-            for j in range(1, lons):
-                stat(parts, j).wait_recv()
-            each_inner(scale)
-            tiles(0, deep, lambda at: scale(rows, at))
-        else:
-            for j in range(1, lons):
-                stat(k - 1, j).wait_recv()
-            tiles(*spans[k - 1], lambda at: scale(1, at))
+
+        def col(c, _):
+            edge[c, pl.ds(at, span)] += 0.1 * field[t, 0, c + 1, pl.ds(PAD + at, span)]
+            return 0
+        lax.fori_loop(0, cols, col, 0)
+
+    for s in range(STEPS - 1):
+        for k in range(len(coarse)):
+            face(s, k).wait_send()
     for s in range(STEPS):
-        for k in range(len(chunks(s))):
-            face(s, k).wait_send()
         wait_sides_sent(s)
     for j in range(1, lons):
-        stat(parts - 1, j).wait_recv()
-    tiles(*spans[parts - 1], lambda at: scale(1, at))
-    for j in range(1, lons):
-        for part in range(parts + 1):
-            stat(part, j).wait_send()
-
-
-def writer(scaled, dens, out_scaled, out_dens, sems):
+        stat(j).wait_send()
+    add_face(0)
+    face(t, 0).wait_send()
+
+    @pl.when(late)
+    def _():
+        for k in range(1, len(fine) - 1):
+            add_face(k)
+        for k in range(1, len(fine) - 1):
+            face(t, k).wait_send()
+
+
+def write_inner(scaled, dens, out_scaled, out_dens, token, sems):
+    inner, cols, _, _ = scaled.shape
     copies = []
     for i, (src, dst) in enumerate(((scaled, out_scaled), (dens, out_dens))):
-        for r in range(src.shape[0]):
-            copies.append(pltpu.make_async_copy(src.at[r], dst.at[r], sems.at[i, r]))
+        for r in range(inner):
+            copies.append(pltpu.make_async_copy(
+                src.at[r], dst.at[place(r + 2, inner + 1)], sems.at[i, r]))
+    for copy in copies:
+        copy.start()
+    token[...] = jnp.zeros(token.shape, jnp.float32)
+    for copy in copies:
+        copy.wait()
+
+
+def last_row(lons, edge, front, token, out_scaled, out_dens, other, stats, peers,
+             entered, face_send, face_recv, stat_send, stat_recv):
+    cols, deep, lanes = edge.shape
+    _, fine = split(deep)
+    end = len(fine) - 1
+    lat, lon = lax.axis_index("lat"), lax.axis_index("lon")
+    late = lax.rem(lon, 2)
+    early = 1 - late
+    order = late * lons + lon
+
+    barrier = pltpu.get_barrier_semaphore()
+    signal(barrier, {"lat": 1 - lat})
+    before = 0
+    for j in range(1, lons):
+        there = lax.rem(lon + j, lons)
+        ahead = lax.rem(there, 2) * lons + there < order
+        before += ahead.astype(jnp.int32)
+        pl.when(jnp.logical_not(ahead))(lambda: signal(barrier, {"lon": there}))
+    pl.semaphore_wait(barrier, 1 + before)
+
+    def face(k):
+        at, span = fine[k]
+        return pltpu.make_async_remote_copy(
+            src_ref=front.at[:, pl.ds(at, span)],
+            dst_ref=other.at[:, pl.ds(at, span)],
+            send_sem=face_send.at[k],
+            recv_sem=face_recv.at[k],
+            device_id={"lat": 1 - lat},
+            device_id_type=MESH,
+        )
+
+    def stat(part, j):
+        pick = (slice(None), pl.ds(deep - 8, 8) if part else pl.ds(0, deep - 8))
+        return pltpu.make_async_remote_copy(
+            src_ref=stats.at[pick],
+            dst_ref=peers.at[(j - 1,) + pick],
+            send_sem=stat_send.at[part, j - 1],
+            recv_sem=stat_recv.at[part, j - 1],
+            device_id={"lon": lax.rem(lon + j, lons)},
+            device_id_type=MESH,
+        )
+
+    for k in range(1, end):
+        pl.when(early == 1)(lambda: face(k).start())
+    face(end).start()
+    for j in range(1, lons):
+        there = lax.rem(lon + j, lons)
+        ahead = lax.rem(there, 2) * lons + there < order
+        pl.when(ahead)(lambda: signal(entered, {"lon": there}))
+
+    def finish(at, add):
+        values = [edge[c, pl.ds(at, 8)] for c in range(cols)]
+        if add:
+            values = [v + 0.1 * other[c, pl.ds(at, 8)] for c, v in enumerate(values)]
+        for c in range(cols):
+            out_dens[c, pl.ds(at, 8)] = values[c]
+        total, square = line_sums(values)
+        stats[0, pl.ds(at, 8)] = total
+        stats[1, pl.ds(at, 8)] = square
+
+    def scale(at):
+        pair = [(stats[0, pl.ds(at, 8)], stats[1, pl.ds(at, 8)])]
+        for j in range(lons - 1):
+            pair.append((peers[j, 0, pl.ds(at, 8)], peers[j, 1, pl.ds(at, 8)]))
+        mean, gain = line_scale(pair, cols)
+        for c in range(cols):
+            out_scaled[c, pl.ds(at, 8)] = (out_dens[c, pl.ds(at, 8)] - mean) * gain
+
+    tiles(*fine[0], lambda at: finish(at, False))
+
+    @pl.when(early == 0)
+    def _():
+        for k in range(1, end):
+            tiles(*fine[k], lambda at: finish(at, False))
+
+    @pl.when(early == 1)
+    def _():
+        for k in range(1, end):
+            face(k).wait_recv()
+            tiles(*fine[k], lambda at: finish(at, True))
+
+    pl.when(before < lons - 1)(lambda: pl.semaphore_wait(entered, lons - 1 - before))
+    for j in range(1, lons):
+        stat(0, j).start()
+    face(end).wait_recv()
+    tiles(*fine[end], lambda at: finish(at, True))
+    for j in range(1, lons):
+        stat(1, j).start()
+    for j in range(1, lons):
+        stat(0, j).wait_recv()
+    tiles(0, deep - 8, scale)
+    for k in range(1, end):
+        pl.when(early == 1)(lambda: face(k).wait_send())
+    face(end).wait_send()
+    for j in range(1, lons):
+        stat(1, j).wait_recv()
+    tiles(*fine[end], scale)
+    for part in range(2):
+        for j in range(1, lons):
+            stat(part, j).wait_send()
+
+
+def write_last(scaled, dens, in_scaled, in_dens, out_scaled, out_dens, sems):
+    del in_scaled, in_dens
+    rows, many = out_dens.shape[0], sems.shape[1]
+    step = dens.shape[0] // many
+    copies = []
+    for i, (src, dst) in enumerate(((scaled, out_scaled), (dens, out_dens))):
+        for part in range(many):
+            span = pl.ds(part * step, step)
+            copies.append(pltpu.make_async_copy(
+                src.at[span], dst.at[place(1, rows), span], sems.at[i, part]))
     for copy in copies:
         copy.start()
     for copy in copies:
         copy.wait()
 
 
-def written(scaled, dens):
-    out = jax.ShapeDtypeStruct(dens.shape, dens.dtype)
-    return pl.pallas_call(
-        writer,
-        out_shape=(out, out),
-        in_specs=[pl.BlockSpec(memory_space=pltpu.VMEM)] * 2,
-        out_specs=[pl.BlockSpec(memory_space=pl.ANY)] * 2,
-        scratch_shapes=[pltpu.SemaphoreType.DMA((2, dens.shape[0]))],
-        compiler_params=pltpu.CompilerParams(vmem_limit_bytes=2**20),
-    )(
-        pltpu.with_memory_space_constraint(scaled, pltpu.VMEM),
-        pltpu.with_memory_space_constraint(dens, pltpu.VMEM),
-    )
-
-
-def one_kernel(lons, levs, density, crowding):
+def in_vmem(*arrays):
+    return [pltpu.with_memory_space_constraint(a, pltpu.VMEM) for a in arrays]
+
+
+def all_steps(lons, levs, density, crowding):
     rows, cols, deep, lanes = density.shape
-    half = deep // 2
-    coarse = [(0, half), (half, half)]
-    fine = coarse[:1] + [(half, half - 8), (deep - 8, 8)]
-    parts = len(fine)
+    coarse, fine = split(deep)
     sem = pltpu.SemaphoreType.DMA
     peers = max(lons - 1, 1)
-    out = pltpu.VMEM(density.shape, jnp.float32)
-    return pl.pallas_call(
-        functools.partial(kernel, lons, levs, coarse, fine),
-        out_shape=(out, out),
-        in_specs=[pl.BlockSpec(memory_space=pl.ANY)] * 2,
-        out_specs=[pl.BlockSpec(memory_space=pltpu.VMEM)] * 2,
+    inner = pltpu.VMEM((rows - 1, cols, deep, lanes), jnp.float32)
+    row = pltpu.VMEM((cols, deep, lanes), jnp.float32)
+    any_space = pl.BlockSpec(memory_space=pl.ANY)
+    vmem = pl.BlockSpec(memory_space=pltpu.VMEM)
+    scaled, dens, edge, front = pl.pallas_call(
+        functools.partial(kernel, lons, levs),
+        out_shape=(inner, inner, row, row),
+        in_specs=[any_space] * 2,
+        out_specs=[vmem] * 4,
         scratch_shapes=[
             pltpu.VMEM((STEPS, rows + 1, cols + 2, deep + 2 * PAD, lanes), jnp.float32),
             pltpu.VMEM((rows, cols, deep, lanes), jnp.float32),
-            pltpu.VMEM((rows, 2, deep, lanes), jnp.float32),
-            pltpu.VMEM((peers, rows, 2, deep, lanes), jnp.float32),
+            pltpu.VMEM((rows - 1, 2, deep, lanes), jnp.float32),
+            pltpu.VMEM((peers, rows - 1, 2, deep, lanes), jnp.float32),
             sem((2, rows)),
             sem((len(coarse),)),
-            sem((STEPS, parts)),
-            sem((STEPS, parts)),
+            sem((STEPS, len(fine))),
+            sem((STEPS, len(fine))),
             sem((STEPS, 2)),
             sem((STEPS, 2)),
             sem((STEPS, 2)),
             sem((STEPS, 2)),
-            sem((parts + 1, peers)),
-            sem((parts + 1, peers)),
+            sem((peers,)),
+            sem((peers,)),
         ],
         compiler_params=pltpu.CompilerParams(
             collective_id=0, has_side_effects=True, vmem_limit_bytes=VMEM_LIMIT
         ),
     )(density, crowding)
+
+    out = jax.ShapeDtypeStruct(density.shape, density.dtype)
+    out_scaled, out_dens, token = pl.pallas_call(
+        write_inner,
+        out_shape=(out, out, pltpu.VMEM((8, lanes), jnp.float32)),
+        in_specs=[vmem] * 2,
+        out_specs=[pl.BlockSpec(memory_space=pltpu.HBM)] * 2 + [vmem],
+        scratch_shapes=[sem((2, rows - 1))],
+        compiler_params=pltpu.CompilerParams(vmem_limit_bytes=2**20),
+    )(*in_vmem(scaled, dens))
+
+    row_scaled, row_dens = pl.pallas_call(
+        functools.partial(last_row, lons),
+        out_shape=(row, row),
+        in_specs=[vmem] * 3,
+        out_specs=[vmem] * 2,
+        scratch_shapes=[
+            pltpu.VMEM((cols, deep, lanes), jnp.float32),
+            pltpu.VMEM((2, deep, lanes), jnp.float32),
+            pltpu.VMEM((peers, 2, deep, lanes), jnp.float32),
+            pltpu.SemaphoreType.REGULAR,
+            sem((len(fine),)),
+            sem((len(fine),)),
+            sem((2, peers)),
+            sem((2, peers)),
+        ],
+        compiler_params=pltpu.CompilerParams(
+            collective_id=1, has_side_effects=True, vmem_limit_bytes=8 * 2**20
+        ),
+    )(*in_vmem(edge, front, token))
+
+    hbm = pl.BlockSpec(memory_space=pltpu.HBM)
+    return pl.pallas_call(
+        write_last,
+        out_shape=(out, out),
+        in_specs=[vmem] * 2 + [hbm] * 2,
+        out_specs=[hbm] * 2,
+        input_output_aliases={2: 0, 3: 1},
+        scratch_shapes=[sem((2, 4 if cols % 4 == 0 else 1))],
+        compiler_params=pltpu.CompilerParams(vmem_limit_bytes=2**20),
+    )(*in_vmem(row_scaled, row_dens), out_scaled, out_dens)
 
 
 VMEM_LIMIT = 44 * 2**20
@@ -395,7 +586,7 @@
         )
         fits = lats == 2 and rows > 1 and lanes == 128 and deep % 32 == 0 and 4 * words < VMEM_LIMIT
         if fits:
-            return tuple(written(*one_kernel(lons, levs, density, crowding)))
+            return tuple(all_steps(lons, levs, density, crowding))
         return general(density, crowding)
 
     spec = P(("trial", "lat"), "lon", "lev", None)

time: 101 us -> 100 us (0.990)
    pallas_call x2 -> x4, Pallas kernels: 99.6 us -> 99.1 us  [the longest x1 85.8 us: all_steps(): pl.pallas_call(functools.partial(kernel, lons, levs), out_shape=(inner, i...]
where the time goes in v1:
time: 100 us; the launch traced here: 99.8 us
  Pallas kernels  99.1 us (99%)
    pallas_call x1, Pallas kernels, all_steps(): pl.pallas_call(functools.partial(kernel, lons, levs), out_shape=(inner, i...  85.8 us
    pallas_call x1, Pallas kernels, all_steps(): pl.pallas_call(functools.partial(last_row, lons), out_shape=(row, row), i...  9.19 us
    pallas_call x1, Pallas kernels, all_steps(): pl.pallas_call(write_inner, out_shape=(out, out, pltpu.VMEM((8, lanes), j...  2.73 us

profile of v1, /device:TPU:1, one launch (start us, length us, event | category | flops | bytes accessed | tf_op | source)
XLA Modules:
  0.0 99.8 jit_solution(16426234624349760555)
XLA Ops:
  0.6 85.8 %shard_map.41 = (f32[3,16,128,128]{3,2,1,0:T(8,128)S(1)}, f32[3,16,128,128]{3,2,1,0:T(8,128)S(1)}, f32[16,128,128]{2,1,0:T(8,128)S(1)}, f32[16,128,128]{2,1,0:T(8,128)S(1)}) custom-call(f32[4,16,128,128]{3,2,1,0:T(8,128)} %dens.1, f32[4,16,128,128]{3,2,1,0:T(8,128)} %crowd.1), custom_call_target="tpu_custom_call" | custom-call | tf_op jit(solution)/shard_map/pallas_call | solution.py:506
  86.5 2.7 %shard_map.42 = (f32[4,16,128,128]{3,2,1,0:T(8,128)}, f32[4,16,128,128]{3,2,1,0:T(8,128)}, f32[8,128]{1,0:T(8,128)S(1)}) custom-call(f32[3,16,128,128]{3,2,1,0:T(8,128)S(1)} %get-tuple-element.13.scaled, f32[3,16,128,128]{3,2,1,0:T(8,128)S(1)} %get-tuple-element.14.dens), custom_call_target="tpu_custom_call" | custom-call | tf_op jit(solution)/shard_map/pallas_call | solution.py:533
  89.2 9.2 %shard_map.43 = (f32[16,128,128]{2,1,0:T(8,128)S(1)}, f32[16,128,128]{2,1,0:T(8,128)S(1)}) custom-call(f32[16,128,128]{2,1,0:T(8,128)S(1)} %get-tuple-element.11.edge, f32[16,128,128]{2,1,0:T(8,128)S(1)} %get-tuple-element.12.front, f32[8,128]{1,0:T(8,128)S(1)} %get-tuple-element.15.token), custom_call_target="tpu_custom_call" | custom-call | tf_op jit(solution)/shard_map/pallas_call | solution.py:542
  98.4 1.4 %shard_map.44 = (f32[4,16,128,128]{3,2,1,0:T(8,128)}, f32[4,16,128,128]{3,2,1,0:T(8,128)}) custom-call(f32[16,128,128]{2,1,0:T(8,128)S(1)} %get-tuple-element.16.scaled, f32[16,128,128]{2,1,0:T(8,128)S(1)} %get-tuple-element.17.dens, f32[4,16,128,128]{3,2,1,0:T(8,128)} %get-tuple-element.18.in_scaled, ...), custom_call_target="tpu_custom_call", output_to_operand_aliasing={{0}: (2, {}), {1}: (3, {})} | custom-call | tf_op jit(solution)/shard_map/pallas_call | solution.py:563

commit v2 on v1

--- a/solution.py
+++ b/solution.py
@@ -77,9 +77,9 @@
 
 
 def split(deep):
-    half, first = deep // 2, max(8, deep // 32 * 8)
+    half, first, late = deep // 2, max(8, 3 * deep // 64 * 8), max(8, 3 * deep // 128 * 8)
     coarse = [(0, half), (half, half)]
-    fine = [(0, first), (first, half - first), (half, half - 8), (deep - 8, 8)]
+    fine = [(0, first), (first, deep - 8 - late - first), (deep - 8 - late, late), (deep - 8, 8)]
     return coarse, fine
 
 
@@ -286,8 +286,8 @@
         for k in range(len(coarse)):
             face(t, k).wait_recv()
             advance_row(t, 1, *coarse[k], False)
-            for j, (at, _) in enumerate(chunks(t + 1)):
-                if coarse[k][0] <= at < sum(coarse[k]):
+            for j, chunk in enumerate(chunks(t + 1)):
+                if coarse[k][0] < sum(chunk) <= sum(coarse[k]):
                     start_face(t + 1, j)
         start_sides(t + 1)
 
@@ -377,6 +377,7 @@
     cols, deep, lanes = edge.shape
     _, fine = split(deep)
     end = len(fine) - 1
+    spans = [(0, sum(fine[1]))] + fine[2:]
     lat, lon = lax.axis_index("lat"), lax.axis_index("lon")
     late = lax.rem(lon, 2)
     early = 1 - late
@@ -404,7 +405,7 @@
         )
 
     def stat(part, j):
-        pick = (slice(None), pl.ds(deep - 8, 8) if part else pl.ds(0, deep - 8))
+        pick = (slice(None), pl.ds(*spans[part]))
         return pltpu.make_async_remote_copy(
             src_ref=stats.at[pick],
             dst_ref=peers.at[(j - 1,) + pick],
@@ -441,35 +442,32 @@
             out_scaled[c, pl.ds(at, 8)] = (out_dens[c, pl.ds(at, 8)] - mean) * gain
 
     tiles(*fine[0], lambda at: finish(at, False))
-
-    @pl.when(early == 0)
-    def _():
-        for k in range(1, end):
-            tiles(*fine[k], lambda at: finish(at, False))
-
-    @pl.when(early == 1)
-    def _():
-        for k in range(1, end):
+    for k in range(1, end + 1):
+        if k < end:
+            pl.when(early == 0)(lambda: tiles(*fine[k], lambda at: finish(at, False)))
+
+            @pl.when(early == 1)
+            def _():
+                face(k).wait_recv()
+                tiles(*fine[k], lambda at: finish(at, True))
+        else:
             face(k).wait_recv()
             tiles(*fine[k], lambda at: finish(at, True))
-
-    pl.when(before < lons - 1)(lambda: pl.semaphore_wait(entered, lons - 1 - before))
-    for j in range(1, lons):
-        stat(0, j).start()
-    face(end).wait_recv()
-    tiles(*fine[end], lambda at: finish(at, True))
-    for j in range(1, lons):
-        stat(1, j).start()
-    for j in range(1, lons):
-        stat(0, j).wait_recv()
-    tiles(0, deep - 8, scale)
+        if k == 1:
+            pl.when(before < lons - 1)(lambda: pl.semaphore_wait(entered, lons - 1 - before))
+        for j in range(1, lons):
+            stat(k - 1, j).start()
+        if k > 1:
+            for j in range(1, lons):
+                stat(k - 2, j).wait_recv()
+            tiles(*spans[k - 2], scale)
     for k in range(1, end):
         pl.when(early == 1)(lambda: face(k).wait_send())
     face(end).wait_send()
     for j in range(1, lons):
-        stat(1, j).wait_recv()
-    tiles(*fine[end], scale)
-    for part in range(2):
+        stat(end - 1, j).wait_recv()
+    tiles(*spans[end - 1], scale)
+    for part in range(len(spans)):
         for j in range(1, lons):
             stat(part, j).wait_send()
 
@@ -551,8 +549,8 @@
             pltpu.SemaphoreType.REGULAR,
             sem((len(fine),)),
             sem((len(fine),)),
-            sem((2, peers)),
-            sem((2, peers)),
+            sem((len(fine) - 1, peers)),
+            sem((len(fine) - 1, peers)),
         ],
         compiler_params=pltpu.CompilerParams(
             collective_id=1, has_side_effects=True, vmem_limit_bytes=8 * 2**20

time: 100 us -> 100 us (level)
    pallas_call x1, Pallas kernels: 9.19 us -> 7.7 us  [all_steps(): pl.pallas_call(functools.partial(last_row, lons), out_shape=(row, row), i...]
    pallas_call x1, Pallas kernels: 85.8 us -> 87.2 us  [all_steps(): pl.pallas_call(functools.partial(kernel, lons, levs), out_shape=(inner, i...]
where the time goes in v2:
time: 100 us; the launch traced here: 99.7 us
  Pallas kernels  99 us (99%)
    pallas_call x1, Pallas kernels, all_steps(): pl.pallas_call(functools.partial(kernel, lons, levs), out_shape=(inner, i...  87.2 us
    pallas_call x1, Pallas kernels, all_steps(): pl.pallas_call(functools.partial(last_row, lons), out_shape=(row, row), i...  7.7 us
    pallas_call x1, Pallas kernels, all_steps(): pl.pallas_call(write_inner, out_shape=(out, out, pltpu.VMEM((8, lanes), j...  2.73 us

profile of v2, /device:TPU:1, one launch (start us, length us, event | category | flops | bytes accessed | tf_op | source)
XLA Modules:
  0.0 99.7 jit_solution(5087785269164715579)
XLA Ops:
  0.6 87.2 %shard_map.41 = (f32[3,16,128,128]{3,2,1,0:T(8,128)S(1)}, f32[3,16,128,128]{3,2,1,0:T(8,128)S(1)}, f32[16,128,128]{2,1,0:T(8,128)S(1)}, f32[16,128,128]{2,1,0:T(8,128)S(1)}) custom-call(f32[4,16,128,128]{3,2,1,0:T(8,128)} %dens.1, f32[4,16,128,128]{3,2,1,0:T(8,128)} %crowd.1), custom_call_target="tpu_custom_call" | custom-call | tf_op jit(solution)/shard_map/pallas_call | solution.py:504
  87.9 2.7 %shard_map.42 = (f32[4,16,128,128]{3,2,1,0:T(8,128)}, f32[4,16,128,128]{3,2,1,0:T(8,128)}, f32[8,128]{1,0:T(8,128)S(1)}) custom-call(f32[3,16,128,128]{3,2,1,0:T(8,128)S(1)} %get-tuple-element.13.scaled, f32[3,16,128,128]{3,2,1,0:T(8,128)S(1)} %get-tuple-element.14.dens), custom_call_target="tpu_custom_call" | custom-call | tf_op jit(solution)/shard_map/pallas_call | solution.py:531
  90.6 7.7 %shard_map.43 = (f32[16,128,128]{2,1,0:T(8,128)S(1)}, f32[16,128,128]{2,1,0:T(8,128)S(1)}) custom-call(f32[16,128,128]{2,1,0:T(8,128)S(1)} %get-tuple-element.11.edge, f32[16,128,128]{2,1,0:T(8,128)S(1)} %get-tuple-element.12.front, f32[8,128]{1,0:T(8,128)S(1)} %get-tuple-element.15.token), custom_call_target="tpu_custom_call" | custom-call | tf_op jit(solution)/shard_map/pallas_call | solution.py:540
  98.3 1.4 %shard_map.44 = (f32[4,16,128,128]{3,2,1,0:T(8,128)}, f32[4,16,128,128]{3,2,1,0:T(8,128)}) custom-call(f32[16,128,128]{2,1,0:T(8,128)S(1)} %get-tuple-element.16.scaled, f32[16,128,128]{2,1,0:T(8,128)S(1)} %get-tuple-element.17.dens, f32[4,16,128,128]{3,2,1,0:T(8,128)} %get-tuple-element.18.in_scaled, ...), custom_call_target="tpu_custom_call", output_to_operand_aliasing={{0}: (2, {}), {1}: (3, {})} | custom-call | tf_op jit(solution)/shard_map/pallas_call | solution.py:561

commit v3 on v2

--- a/solution.py
+++ b/solution.py
@@ -77,7 +77,7 @@
 
 
 def split(deep):
-    half, first, late = deep // 2, max(8, 3 * deep // 64 * 8), max(8, 3 * deep // 128 * 8)
+    half, first, late = deep // 2, max(8, deep // 32 * 8), max(8, 3 * deep // 128 * 8)
     coarse = [(0, half), (half, half)]
     fine = [(0, first), (first, deep - 8 - late - first), (deep - 8 - late, late), (deep - 8, 8)]
     return coarse, fine
@@ -117,7 +117,7 @@
     lat, lon, lev = lax.axis_index("lat"), lax.axis_index("lon"), lax.axis_index("lev")
     has_left, has_right = lon > 0, lon < lons - 1
     has_down, has_up = lev > 0, lev < levs - 1
-    late = lax.rem(lon, 2) == 1
+    late = lax.rem(lon, 2) == 0
 
     first = [
         pltpu.make_async_copy(
@@ -161,58 +161,63 @@
             device_id_type=MESH,
         )
 
-    def lon_side(t, right):
+    bands = (pl.ds(1, 1), pl.ds(2, rows - 1))
+
+    def lon_side(t, band, right):
         own, theirs = (cols, 0) if right else (1, cols + 1)
-        span = pl.ds(1, rows)
+        span = bands[band]
         return pltpu.make_async_remote_copy(
             src_ref=field.at[t, span, own, pl.ds(PAD, deep)],
             dst_ref=field.at[t, span, theirs, pl.ds(PAD, deep)],
-            send_sem=lon_send.at[t, int(right)],
-            recv_sem=lon_recv.at[t, int(right)],
+            send_sem=lon_send.at[t, band, int(right)],
+            recv_sem=lon_recv.at[t, band, int(right)],
             device_id={"lon": lon + 1 if right else lon - 1},
             device_id_type=MESH,
         )
 
-    def lev_side(t, up):
+    def lev_side(t, band, up):
         own, theirs = (PAD + deep - 1, PAD - 1) if up else (PAD, PAD + deep)
-        span = (pl.ds(1, rows), pl.ds(1, cols))
+        span = (bands[band], pl.ds(1, cols))
         return pltpu.make_async_remote_copy(
             src_ref=field.at[t, span[0], span[1], pl.ds(own, 1)],
             dst_ref=field.at[t, span[0], span[1], pl.ds(theirs, 1)],
-            send_sem=lev_send.at[t, int(up)],
-            recv_sem=lev_recv.at[t, int(up)],
+            send_sem=lev_send.at[t, band, int(up)],
+            recv_sem=lev_recv.at[t, band, int(up)],
             device_id={"lev": lev + 1 if up else lev - 1},
             device_id_type=MESH,
         )
 
-    def sides(t, act):
+    def sides(t, band, act):
         if lons > 1:
-            pl.when(has_right)(lambda: act(lon_side(t, True), 1))
-            pl.when(has_left)(lambda: act(lon_side(t, False), 0))
+            pl.when(has_right)(lambda: act(lon_side(t, band, True)))
+            pl.when(has_left)(lambda: act(lon_side(t, band, False)))
         if levs > 1:
-            pl.when(has_up)(lambda: act(lev_side(t, True), 1))
-            pl.when(has_down)(lambda: act(lev_side(t, False), 0))
-
-    def start_sides(t):
-        sides(t, lambda copy, _: copy.start())
-
-    def wait_sides_sent(t):
-        sides(t, lambda copy, _: copy.wait_send())
-
-    def wait_sides(t):
+            pl.when(has_up)(lambda: act(lev_side(t, band, True)))
+            pl.when(has_down)(lambda: act(lev_side(t, band, False)))
+
+    def start_sides(t, band):
+        sides(t, band, lambda copy: copy.start())
+
+    def wait_sides_sent(t, band):
+        sides(t, band, lambda copy: copy.wait_send())
+
+    def wait_sides(t, band):
         if lons > 1:
-            pl.when(has_left)(lambda: lon_side(t, True).wait_recv())
-            pl.when(has_right)(lambda: lon_side(t, False).wait_recv())
+            pl.when(has_left)(lambda: lon_side(t, band, True).wait_recv())
+            pl.when(has_right)(lambda: lon_side(t, band, False).wait_recv())
         if levs > 1:
-            pl.when(has_down)(lambda: lev_side(t, True).wait_recv())
-            pl.when(has_up)(lambda: lev_side(t, False).wait_recv())
-
-    def stat(j):
+            pl.when(has_down)(lambda: lev_side(t, band, True).wait_recv())
+            pl.when(has_up)(lambda: lev_side(t, band, False).wait_recv())
+
+    stat_rows = (pl.ds(0, 1), pl.ds(1, rows - 2))
+    groups = range(2 if rows > 2 else 1)
+
+    def stat(group, j):
         return pltpu.make_async_remote_copy(
-            src_ref=stats,
-            dst_ref=peers.at[j - 1],
-            send_sem=stat_send.at[j - 1],
-            recv_sem=stat_recv.at[j - 1],
+            src_ref=stats.at[stat_rows[group]],
+            dst_ref=peers.at[j - 1, stat_rows[group]],
+            send_sem=stat_send.at[group, j - 1],
+            recv_sem=stat_recv.at[group, j - 1],
             device_id={"lon": lax.rem(lon + j, lons)},
             device_id_type=MESH,
         )
@@ -244,7 +249,8 @@
 
     for copy in loads:
         copy.wait()
-    start_sides(0)
+    start_sides(0, 1)
+    start_sides(0, 0)
 
     def cell(t, r, c, at, span, below, above):
         here = field[t, r, c, pl.ds(PAD + at, span)]
@@ -274,28 +280,8 @@
         else:
             face(t, k).start()
 
-    for t in range(STEPS - 1):
-        wait_sides(t)
-
-        def inner(r, _, t=t):
-            advance_row(t, r, 0, deep, False)
-            return 0
-
-        lax.fori_loop(2, rows, inner, 0)
-        advance_row(t, rows, 0, deep, True)
-        for k in range(len(coarse)):
-            face(t, k).wait_recv()
-            advance_row(t, 1, *coarse[k], False)
-            for j, chunk in enumerate(chunks(t + 1)):
-                if coarse[k][0] < sum(chunk) <= sum(coarse[k]):
-                    start_face(t + 1, j)
-        start_sides(t + 1)
-
-    t = STEPS - 1
-    wait_sides(t)
-
     def finish(r, at, last):
-        values = [cell(t, r, c, at, 8, True, not last) for c in range(1, cols + 1)]
+        values = [cell(STEPS - 1, r, c, at, 8, True, not last) for c in range(1, cols + 1)]
         for c in range(cols):
             out_dens[r - 2, c, pl.ds(at, 8)] = values[c]
         total, square = line_sums(values)
@@ -310,26 +296,59 @@
         for c in range(cols):
             out_scaled[r - 2, c, pl.ds(at, 8)] = (out_dens[r - 2, c, pl.ds(at, 8)] - mean) * gain
 
-    def each_inner(act):
+    def each_row(first, last, act):
         def row(r, _):
             tiles(0, deep, lambda at: act(r, at))
             return 0
-        lax.fori_loop(2, rows, row, 0)
-
-    each_inner(lambda r, at: finish(r, at, False))
-    tiles(0, deep, lambda at: finish(rows, at, True))
-    for j in range(1, lons):
-        stat(j).start()
+        lax.fori_loop(first, last, row, 0)
+
+    def send_sums(group):
+        for j in range(1, lons):
+            stat(group, j).start()
+
+    def wait_sums(group):
+        for j in range(1, lons):
+            stat(group, j).wait_recv()
+
+    for t in range(STEPS - 1):
+        wait_sides(t, 1)
+
+        def inner(r, _, t=t):
+            advance_row(t, r, 0, deep, False)
+            return 0
+
+        lax.fori_loop(2, rows, inner, 0)
+        advance_row(t, rows, 0, deep, True)
+        start_sides(t + 1, 1)
+        if t == STEPS - 2:
+            wait_sides(t + 1, 1)
+            if rows > 2:
+                each_row(3, rows, lambda r, at: finish(r, at, False))
+                tiles(0, deep, lambda at: finish(rows, at, True))
+                send_sums(1)
+                wait_sums(1)
+                each_row(3, rows + 1, scale)
+        wait_sides(t, 0)
+        for k in range(len(coarse)):
+            face(t, k).wait_recv()
+            advance_row(t, 1, *coarse[k], False)
+            for j, chunk in enumerate(chunks(t + 1)):
+                if coarse[k][0] < sum(chunk) <= sum(coarse[k]):
+                    start_face(t + 1, j)
+        start_sides(t + 1, 0)
+
+    t = STEPS - 1
+    tiles(0, deep, lambda at: finish(2, at, rows == 2))
+    send_sums(0)
+    wait_sides(t, 0)
 
     def base(c, _):
         edge[c - 1] = cell(t, 1, c, 0, deep, False, True)
         return 0
 
     lax.fori_loop(1, cols + 1, base, 0)
-    for j in range(1, lons):
-        stat(j).wait_recv()
-    each_inner(scale)
-    tiles(0, deep, lambda at: scale(rows, at))
+    wait_sums(0)
+    tiles(0, deep, lambda at: scale(2, at))
 
     def add_face(k):
         at, span = fine[k]
@@ -344,9 +363,11 @@
         for k in range(len(coarse)):
             face(s, k).wait_send()
     for s in range(STEPS):
-        wait_sides_sent(s)
-    for j in range(1, lons):
-        stat(j).wait_send()
+        for band in range(2):
+            wait_sides_sent(s, band)
+    for group in groups:
+        for j in range(1, lons):
+            stat(group, j).wait_send()
     add_face(0)
     face(t, 0).wait_send()
 
@@ -358,13 +379,14 @@
             face(t, k).wait_send()
 
 
-def write_inner(scaled, dens, out_scaled, out_dens, token, sems):
+def write_inner(scaled, dens, edge, out_scaled, out_dens, token, sems):
     inner, cols, _, _ = scaled.shape
     copies = []
     for i, (src, dst) in enumerate(((scaled, out_scaled), (dens, out_dens))):
         for r in range(inner):
             copies.append(pltpu.make_async_copy(
                 src.at[r], dst.at[place(r + 2, inner + 1)], sems.at[i, r]))
+    copies.append(pltpu.make_async_copy(edge, out_dens.at[place(1, inner + 1)], sems.at[1, inner]))
     for copy in copies:
         copy.start()
     token[...] = jnp.zeros(token.shape, jnp.float32)
@@ -379,8 +401,8 @@
     end = len(fine) - 1
     spans = [(0, sum(fine[1]))] + fine[2:]
     lat, lon = lax.axis_index("lat"), lax.axis_index("lon")
-    late = lax.rem(lon, 2)
-    early = 1 - late
+    early = lax.rem(lon, 2)
+    late = 1 - early
     order = late * lons + lon
 
     barrier = pltpu.get_barrier_semaphore()
@@ -388,7 +410,7 @@
     before = 0
     for j in range(1, lons):
         there = lax.rem(lon + j, lons)
-        ahead = lax.rem(there, 2) * lons + there < order
+        ahead = (1 - lax.rem(there, 2)) * lons + there < order
         before += ahead.astype(jnp.int32)
         pl.when(jnp.logical_not(ahead))(lambda: signal(barrier, {"lon": there}))
     pl.semaphore_wait(barrier, 1 + before)
@@ -420,7 +442,7 @@
     face(end).start()
     for j in range(1, lons):
         there = lax.rem(lon + j, lons)
-        ahead = lax.rem(there, 2) * lons + there < order
+        ahead = (1 - lax.rem(there, 2)) * lons + there < order
         pl.when(ahead)(lambda: signal(entered, {"lon": there}))
 
     def finish(at, add):
@@ -474,18 +496,35 @@
 
 def write_last(scaled, dens, in_scaled, in_dens, out_scaled, out_dens, sems):
     del in_scaled, in_dens
-    rows, many = out_dens.shape[0], sems.shape[1]
-    step = dens.shape[0] // many
-    copies = []
-    for i, (src, dst) in enumerate(((scaled, out_scaled), (dens, out_dens))):
-        for part in range(many):
-            span = pl.ds(part * step, step)
-            copies.append(pltpu.make_async_copy(
-                src.at[span], dst.at[place(1, rows), span], sems.at[i, part]))
-    for copy in copies:
-        copy.start()
-    for copy in copies:
-        copy.wait()
+    rows, many = out_dens.shape[0], sems.shape[1] - 1
+    cols, deep, _ = dens.shape
+    late = lax.rem(lax.axis_index("lon"), 2) == 0
+
+    def copies(src, dst, i, known):
+        if known:
+            span = pl.ds(deep - 8, 8)
+            return [pltpu.make_async_copy(
+                src.at[:, span], dst.at[place(1, rows), :, span], sems.at[i, many])]
+        step = cols // many
+        return [
+            pltpu.make_async_copy(
+                src.at[pl.ds(part * step, step)],
+                dst.at[place(1, rows), pl.ds(part * step, step)],
+                sems.at[i, part])
+            for part in range(many)
+        ]
+
+    def each(act):
+        for copy in copies(scaled, out_scaled, 0, False):
+            act(copy)
+        for known in (False, True):
+            @pl.when(late == known)
+            def _():
+                for copy in copies(dens, out_dens, 1, known):
+                    act(copy)
+
+    each(lambda copy: copy.start())
+    each(lambda copy: copy.wait())
 
 
 def in_vmem(*arrays):
@@ -515,12 +554,12 @@
             sem((len(coarse),)),
             sem((STEPS, len(fine))),
             sem((STEPS, len(fine))),
-            sem((STEPS, 2)),
-            sem((STEPS, 2)),
-            sem((STEPS, 2)),
-            sem((STEPS, 2)),
-            sem((peers,)),
-            sem((peers,)),
+            sem((STEPS, 2, 2)),
+            sem((STEPS, 2, 2)),
+            sem((STEPS, 2, 2)),
+            sem((STEPS, 2, 2)),
+            sem((2, peers)),
+            sem((2, peers)),
         ],
         compiler_params=pltpu.CompilerParams(
             collective_id=0, has_side_effects=True, vmem_limit_bytes=VMEM_LIMIT
@@ -531,11 +570,11 @@
     out_scaled, out_dens, token = pl.pallas_call(
         write_inner,
         out_shape=(out, out, pltpu.VMEM((8, lanes), jnp.float32)),
-        in_specs=[vmem] * 2,
+        in_specs=[vmem] * 3,
         out_specs=[pl.BlockSpec(memory_space=pltpu.HBM)] * 2 + [vmem],
-        scratch_shapes=[sem((2, rows - 1))],
+        scratch_shapes=[sem((2, rows))],
         compiler_params=pltpu.CompilerParams(vmem_limit_bytes=2**20),
-    )(*in_vmem(scaled, dens))
+    )(*in_vmem(scaled, dens, edge))
 
     row_scaled, row_dens = pl.pallas_call(
         functools.partial(last_row, lons),
@@ -564,7 +603,7 @@
         in_specs=[vmem] * 2 + [hbm] * 2,
         out_specs=[hbm] * 2,
         input_output_aliases={2: 0, 3: 1},
-        scratch_shapes=[sem((2, 4 if cols % 4 == 0 else 1))],
+        scratch_shapes=[sem((2, 5 if cols % 4 == 0 else 2))],
         compiler_params=pltpu.CompilerParams(vmem_limit_bytes=2**20),
     )(*in_vmem(row_scaled, row_dens), out_scaled, out_dens)
 

time: 100 us -> 99.2 us (level)
    pallas_call x1, Pallas kernels: 87.2 us -> 77.6 us  [all_steps(): pl.pallas_call(functools.partial(kernel, lons, levs), out_shape=(inner, i...]
    pallas_call x1, Pallas kernels: 7.7 us -> 16.3 us  [all_steps(): pl.pallas_call(functools.partial(last_row, lons), out_shape=(row, row), i...]
where the time goes in v3:
time: 99.2 us; the launch traced here: 99 us
  Pallas kernels  98.4 us (99%)
    pallas_call x1, Pallas kernels, all_steps(): pl.pallas_call(functools.partial(kernel, lons, levs), out_shape=(inner, i...  77.6 us
    pallas_call x1, Pallas kernels, all_steps(): pl.pallas_call(functools.partial(last_row, lons), out_shape=(row, row), i...  16.3 us
    pallas_call x1, Pallas kernels, all_steps(): pl.pallas_call(write_inner, out_shape=(out, out, pltpu.VMEM((8, lanes), j...  3.06 us

profile of v3, /device:TPU:1, one launch (start us, length us, event | category | flops | bytes accessed | tf_op | source)
XLA Modules:
  0.0 99.0 jit_solution(10650413822255952090)
XLA Ops:
  0.6 77.6 %shard_map.41 = (f32[3,16,128,128]{3,2,1,0:T(8,128)S(1)}, f32[3,16,128,128]{3,2,1,0:T(8,128)S(1)}, f32[16,128,128]{2,1,0:T(8,128)S(1)}, f32[16,128,128]{2,1,0:T(8,128)S(1)}) custom-call(f32[4,16,128,128]{3,2,1,0:T(8,128)} %dens.1, f32[4,16,128,128]{3,2,1,0:T(8,128)} %crowd.1), custom_call_target="tpu_custom_call" | custom-call | tf_op jit(solution)/shard_map/pallas_call | solution.py:543
  78.2 3.1 %shard_map.42 = (f32[4,16,128,128]{3,2,1,0:T(8,128)}, f32[4,16,128,128]{3,2,1,0:T(8,128)}, f32[8,128]{1,0:T(8,128)S(1)}) custom-call(f32[3,16,128,128]{3,2,1,0:T(8,128)S(1)} %get-tuple-element.13.scaled, f32[3,16,128,128]{3,2,1,0:T(8,128)S(1)} %get-tuple-element.14.dens, f32[16,128,128]{2,1,0:T(8,128)S(1)} %get-tuple-element.11.edge), custom_call_target="tpu_custom_call" | custom-call | tf_op jit(solution)/shard_map/pallas_call | solution.py:570
  81.3 16.3 %shard_map.43 = (f32[16,128,128]{2,1,0:T(8,128)S(1)}, f32[16,128,128]{2,1,0:T(8,128)S(1)}) custom-call(f32[16,128,128]{2,1,0:T(8,128)S(1)} %get-tuple-element.11.edge, f32[16,128,128]{2,1,0:T(8,128)S(1)} %get-tuple-element.12.front, f32[8,128]{1,0:T(8,128)S(1)} %get-tuple-element.15.token), custom_call_target="tpu_custom_call" | custom-call | tf_op jit(solution)/shard_map/pallas_call | solution.py:579
  97.6 1.4 %shard_map.44 = (f32[4,16,128,128]{3,2,1,0:T(8,128)}, f32[4,16,128,128]{3,2,1,0:T(8,128)}) custom-call(f32[16,128,128]{2,1,0:T(8,128)S(1)} %get-tuple-element.16.scaled, f32[16,128,128]{2,1,0:T(8,128)S(1)} %get-tuple-element.17.dens, f32[4,16,128,128]{3,2,1,0:T(8,128)} %get-tuple-element.18.in_scaled, ...), custom_call_target="tpu_custom_call", output_to_operand_aliasing={{0}: (2, {}), {1}: (3, {})} | custom-call | tf_op jit(solution)/shard_map/pallas_call | solution.py:600

commit v4 on v3

--- a/solution.py
+++ b/solution.py
@@ -77,10 +77,12 @@
 
 
 def split(deep):
-    half, first, late = deep // 2, max(8, deep // 32 * 8), max(8, 3 * deep // 128 * 8)
+    half, last = deep // 2, deep - 8
+    first, late = max(8, deep // 32 * 8), max(8, deep // 64 * 8)
+    opening = [(0, 8), (8, half - 8), (half, half)]
     coarse = [(0, half), (half, half)]
-    fine = [(0, first), (first, deep - 8 - late - first), (deep - 8 - late, late), (deep - 8, 8)]
-    return coarse, fine
+    fine = [(0, first), (first, last - late - first), (last - late, late), (last, 8)]
+    return opening, coarse, fine
 
 
 def place(r, rows):
@@ -113,7 +115,7 @@
            field, cap, stats, peers, load_sem, edge_sem, face_send, face_recv,
            lon_send, lon_recv, lev_send, lev_recv, stat_send, stat_recv):
     rows, cols, deep, lanes = dens.shape
-    coarse, fine = split(deep)
+    opening, coarse, fine = split(deep)
     lat, lon, lev = lax.axis_index("lat"), lax.axis_index("lon"), lax.axis_index("lev")
     has_left, has_right = lon > 0, lon < lons - 1
     has_down, has_up = lev > 0, lev < levs - 1
@@ -124,7 +126,7 @@
             dens.at[place(1, rows), :, pl.ds(at, span)],
             field.at[0, 1, pl.ds(1, cols), pl.ds(PAD + at, span)],
             edge_sem.at[k])
-        for k, (at, span) in enumerate(coarse)
+        for k, (at, span) in enumerate(opening)
     ]
     loads = []
     for r in range(1, rows + 1):
@@ -148,7 +150,7 @@
     pl.semaphore_wait(barrier, lons + has_down.astype(jnp.int32) + has_up.astype(jnp.int32))
 
     def chunks(t):
-        return fine if t == STEPS - 1 else coarse
+        return opening if t == 0 else fine if t == STEPS - 1 else coarse
 
     def face(t, k):
         at, span = chunks(t)[k]
@@ -222,7 +224,7 @@
             device_id_type=MESH,
         )
 
-    for k in range(len(coarse)):
+    for k in range(len(opening)):
         first[k].wait()
         face(0, k).start()
 
@@ -273,12 +275,10 @@
         lax.fori_loop(1, cols + 1, col, 0)
 
     def start_face(t, k):
-        if t == STEPS - 1 and k == len(fine) - 1:
-            return
-        if t == STEPS - 1 and k > 0:
+        if t < STEPS - 1 or k == 0:
+            face(t, k).start()
+        elif k == 1:
             pl.when(late)(lambda: face(t, k).start())
-        else:
-            face(t, k).start()
 
     def finish(r, at, last):
         values = [cell(STEPS - 1, r, c, at, 8, True, not last) for c in range(1, cols + 1)]
@@ -329,11 +329,11 @@
                 wait_sums(1)
                 each_row(3, rows + 1, scale)
         wait_sides(t, 0)
-        for k in range(len(coarse)):
+        for k, (at, span) in enumerate(chunks(t)):
             face(t, k).wait_recv()
-            advance_row(t, 1, *coarse[k], False)
+            advance_row(t, 1, at, span, False)
             for j, chunk in enumerate(chunks(t + 1)):
-                if coarse[k][0] < sum(chunk) <= sum(coarse[k]):
+                if at < sum(chunk) <= at + span:
                     start_face(t + 1, j)
         start_sides(t + 1, 0)
 
@@ -360,7 +360,7 @@
         lax.fori_loop(0, cols, col, 0)
 
     for s in range(STEPS - 1):
-        for k in range(len(coarse)):
+        for k in range(len(chunks(s))):
             face(s, k).wait_send()
     for s in range(STEPS):
         for band in range(2):
@@ -373,10 +373,8 @@
 
     @pl.when(late)
     def _():
-        for k in range(1, len(fine) - 1):
-            add_face(k)
-        for k in range(1, len(fine) - 1):
-            face(t, k).wait_send()
+        add_face(1)
+        face(t, 1).wait_send()
 
 
 def write_inner(scaled, dens, edge, out_scaled, out_dens, token, sems):
@@ -397,7 +395,7 @@
 def last_row(lons, edge, front, token, out_scaled, out_dens, other, stats, peers,
              entered, face_send, face_recv, stat_send, stat_recv):
     cols, deep, lanes = edge.shape
-    _, fine = split(deep)
+    _, _, fine = split(deep)
     end = len(fine) - 1
     spans = [(0, sum(fine[1]))] + fine[2:]
     lat, lon = lax.axis_index("lat"), lax.axis_index("lon")
@@ -437,9 +435,9 @@
             device_id_type=MESH,
         )
 
-    for k in range(1, end):
-        pl.when(early == 1)(lambda: face(k).start())
-    face(end).start()
+    pl.when(early == 1)(lambda: face(1).start())
+    for k in range(2, end + 1):
+        face(k).start()
     for j in range(1, lons):
         there = lax.rem(lon + j, lons)
         ahead = (1 - lax.rem(there, 2)) * lons + there < order
@@ -465,7 +463,7 @@
 
     tiles(*fine[0], lambda at: finish(at, False))
     for k in range(1, end + 1):
-        if k < end:
+        if k == 1:
             pl.when(early == 0)(lambda: tiles(*fine[k], lambda at: finish(at, False)))
 
             @pl.when(early == 1)
@@ -483,9 +481,9 @@
             for j in range(1, lons):
                 stat(k - 2, j).wait_recv()
             tiles(*spans[k - 2], scale)
-    for k in range(1, end):
-        pl.when(early == 1)(lambda: face(k).wait_send())
-    face(end).wait_send()
+    pl.when(early == 1)(lambda: face(1).wait_send())
+    for k in range(2, end + 1):
+        face(k).wait_send()
     for j in range(1, lons):
         stat(end - 1, j).wait_recv()
     tiles(*spans[end - 1], scale)
@@ -496,31 +494,28 @@
 
 def write_last(scaled, dens, in_scaled, in_dens, out_scaled, out_dens, sems):
     del in_scaled, in_dens
-    rows, many = out_dens.shape[0], sems.shape[1] - 1
+    rows, many = out_dens.shape[0], sems.shape[1]
     cols, deep, _ = dens.shape
+    _, _, fine = split(deep)
     late = lax.rem(lax.axis_index("lon"), 2) == 0
 
     def copies(src, dst, i, known):
-        if known:
-            span = pl.ds(deep - 8, 8)
-            return [pltpu.make_async_copy(
-                src.at[:, span], dst.at[place(1, rows), :, span], sems.at[i, many])]
         step = cols // many
         return [
             pltpu.make_async_copy(
-                src.at[pl.ds(part * step, step)],
-                dst.at[place(1, rows), pl.ds(part * step, step)],
+                src.at[pl.ds(part * step, step), pl.ds(known, deep - known)],
+                dst.at[place(1, rows), pl.ds(part * step, step), pl.ds(known, deep - known)],
                 sems.at[i, part])
             for part in range(many)
         ]
 
     def each(act):
-        for copy in copies(scaled, out_scaled, 0, False):
+        for copy in copies(scaled, out_scaled, 0, 0):
             act(copy)
-        for known in (False, True):
-            @pl.when(late == known)
+        for moved in range(2):
+            @pl.when(late == moved)
             def _():
-                for copy in copies(dens, out_dens, 1, known):
+                for copy in copies(dens, out_dens, 1, sum(fine[moved])):
                     act(copy)
 
     each(lambda copy: copy.start())
@@ -533,7 +528,7 @@
 
 def all_steps(lons, levs, density, crowding):
     rows, cols, deep, lanes = density.shape
-    coarse, fine = split(deep)
+    opening, coarse, fine = split(deep)
     sem = pltpu.SemaphoreType.DMA
     peers = max(lons - 1, 1)
     inner = pltpu.VMEM((rows - 1, cols, deep, lanes), jnp.float32)
@@ -551,7 +546,7 @@
             pltpu.VMEM((rows - 1, 2, deep, lanes), jnp.float32),
             pltpu.VMEM((peers, rows - 1, 2, deep, lanes), jnp.float32),
             sem((2, rows)),
-            sem((len(coarse),)),
+            sem((len(opening),)),
             sem((STEPS, len(fine))),
             sem((STEPS, len(fine))),
             sem((STEPS, 2, 2)),
@@ -603,7 +598,7 @@
         in_specs=[vmem] * 2 + [hbm] * 2,
         out_specs=[hbm] * 2,
         input_output_aliases={2: 0, 3: 1},
-        scratch_shapes=[sem((2, 5 if cols % 4 == 0 else 2))],
+        scratch_shapes=[sem((2, 4 if cols % 4 == 0 else 1))],
         compiler_params=pltpu.CompilerParams(vmem_limit_bytes=2**20),
     )(*in_vmem(row_scaled, row_dens), out_scaled, out_dens)
 

time: 99.2 us -> 97.8 us (0.986)
  Pallas kernels: 98.4 us -> 97 us
    pallas_call x1, Pallas kernels: 16.3 us -> 15.1 us  [all_steps(): pl.pallas_call(functools.partial(last_row, lons), out_shape=(row, row), i...]
where the time goes in v4:
time: 97.8 us; the launch traced here: 97.6 us
  Pallas kernels  97 us (99%)
    pallas_call x1, Pallas kernels, all_steps(): pl.pallas_call(functools.partial(kernel, lons, levs), out_shape=(inner, i...  77.6 us
    pallas_call x1, Pallas kernels, all_steps(): pl.pallas_call(functools.partial(last_row, lons), out_shape=(row, row), i...  15.1 us
    pallas_call x1, Pallas kernels, all_steps(): pl.pallas_call(write_inner, out_shape=(out, out, pltpu.VMEM((8, lanes), j...  3.06 us

profile of v4, /device:TPU:1, one launch (start us, length us, event | category | flops | bytes accessed | tf_op | source)
XLA Modules:
  0.0 97.6 jit_solution(2456834631810649448)
XLA Ops:
  0.6 77.6 %shard_map.41 = (f32[3,16,128,128]{3,2,1,0:T(8,128)S(1)}, f32[3,16,128,128]{3,2,1,0:T(8,128)S(1)}, f32[16,128,128]{2,1,0:T(8,128)S(1)}, f32[16,128,128]{2,1,0:T(8,128)S(1)}) custom-call(f32[4,16,128,128]{3,2,1,0:T(8,128)} %dens.1, f32[4,16,128,128]{3,2,1,0:T(8,128)} %crowd.1), custom_call_target="tpu_custom_call" | custom-call | tf_op jit(solution)/shard_map/pallas_call | solution.py:538
  78.2 3.1 %shard_map.42 = (f32[4,16,128,128]{3,2,1,0:T(8,128)}, f32[4,16,128,128]{3,2,1,0:T(8,128)}, f32[8,128]{1,0:T(8,128)S(1)}) custom-call(f32[3,16,128,128]{3,2,1,0:T(8,128)S(1)} %get-tuple-element.13.scaled, f32[3,16,128,128]{3,2,1,0:T(8,128)S(1)} %get-tuple-element.14.dens, f32[16,128,128]{2,1,0:T(8,128)S(1)} %get-tuple-element.11.edge), custom_call_target="tpu_custom_call" | custom-call | tf_op jit(solution)/shard_map/pallas_call | solution.py:565
  81.3 15.1 %shard_map.43 = (f32[16,128,128]{2,1,0:T(8,128)S(1)}, f32[16,128,128]{2,1,0:T(8,128)S(1)}) custom-call(f32[16,128,128]{2,1,0:T(8,128)S(1)} %get-tuple-element.11.edge, f32[16,128,128]{2,1,0:T(8,128)S(1)} %get-tuple-element.12.front, f32[8,128]{1,0:T(8,128)S(1)} %get-tuple-element.15.token), custom_call_target="tpu_custom_call" | custom-call | tf_op jit(solution)/shard_map/pallas_call | solution.py:574
  96.3 1.3 %shard_map.44 = (f32[4,16,128,128]{3,2,1,0:T(8,128)}, f32[4,16,128,128]{3,2,1,0:T(8,128)}) custom-call(f32[16,128,128]{2,1,0:T(8,128)S(1)} %get-tuple-element.16.scaled, f32[16,128,128]{2,1,0:T(8,128)S(1)} %get-tuple-element.17.dens, f32[4,16,128,128]{3,2,1,0:T(8,128)} %get-tuple-element.18.in_scaled, ...), custom_call_target="tpu_custom_call", output_to_operand_aliasing={{0}: (2, {}), {1}: (3, {})} | custom-call | tf_op jit(solution)/shard_map/pallas_call | solution.py:595

commit v5 on v4

--- a/solution.py
+++ b/solution.py
@@ -119,7 +119,7 @@
     lat, lon, lev = lax.axis_index("lat"), lax.axis_index("lon"), lax.axis_index("lev")
     has_left, has_right = lon > 0, lon < lons - 1
     has_down, has_up = lev > 0, lev < levs - 1
-    late = lax.rem(lon, 2) == 0
+    late = lax.rem(lon, 2) == 1
 
     first = [
         pltpu.make_async_copy(
@@ -392,56 +392,81 @@
         copy.wait()
 
 
-def last_row(lons, edge, front, token, out_scaled, out_dens, other, stats, peers,
-             entered, face_send, face_recv, stat_send, stat_recv):
+def last_row(lons, edge, front, token, out_scaled, out_dens, *refs):
+    twin = lons == 2
+    tile_base, tile_face, tile_sums = refs[:3] if twin else (None,) * 3
+    (other, stats, peers, entered, face_send, face_recv, stat_send, stat_recv,
+     tile_send, tile_recv) = refs[3:] if twin else refs
     cols, deep, lanes = edge.shape
     _, _, fine = split(deep)
     end = len(fine) - 1
     spans = [(0, sum(fine[1]))] + fine[2:]
+    tail = pl.ds(*fine[end])
     lat, lon = lax.axis_index("lat"), lax.axis_index("lon")
-    early = lax.rem(lon, 2)
-    late = 1 - early
-    order = late * lons + lon
+    late = lax.rem(lon, 2) == 1
+    early = jnp.logical_not(late)
+
+    def ahead(there):
+        return lax.rem(there, 2) * lons + there < lax.rem(lon, 2) * lons + lon
 
     barrier = pltpu.get_barrier_semaphore()
     signal(barrier, {"lat": 1 - lat})
     before = 0
     for j in range(1, lons):
         there = lax.rem(lon + j, lons)
-        ahead = (1 - lax.rem(there, 2)) * lons + there < order
-        before += ahead.astype(jnp.int32)
-        pl.when(jnp.logical_not(ahead))(lambda: signal(barrier, {"lon": there}))
-    pl.semaphore_wait(barrier, 1 + before)
+        before += ahead(there).astype(jnp.int32)
+
+        @pl.when(jnp.logical_not(ahead(there)))
+        def _():
+            signal(barrier, {"lon": there})
+            if twin:
+                signal(barrier, {"lat": 1 - lat, "lon": there})
+    pl.semaphore_wait(barrier, 1 + before * (2 if twin else 1))
+
+    def remote(src, dst, send, recv, where):
+        return pltpu.make_async_remote_copy(
+            src_ref=src, dst_ref=dst, send_sem=send, recv_sem=recv,
+            device_id=where, device_id_type=MESH)
 
     def face(k):
-        at, span = fine[k]
-        return pltpu.make_async_remote_copy(
-            src_ref=front.at[:, pl.ds(at, span)],
-            dst_ref=other.at[:, pl.ds(at, span)],
-            send_sem=face_send.at[k],
-            recv_sem=face_recv.at[k],
-            device_id={"lat": 1 - lat},
-            device_id_type=MESH,
-        )
+        pick = (slice(None), pl.ds(*fine[k]))
+        return remote(front.at[pick], other.at[pick], face_send.at[k], face_recv.at[k],
+                      {"lat": 1 - lat})
+
+    def tile_copy(i):
+        src = (front, front, edge, stats)[i].at[:, tail]
+        dst = (tile_face, tile_face, tile_base, tile_sums)[i]
+        where = {"lat": 1 - lat} if i < 2 else {}
+        if i > 0:
+            where["lon"] = 1 - lon
+        return remote(src, dst, tile_send.at[i], tile_recv.at[i], where)
 
     def stat(part, j):
         pick = (slice(None), pl.ds(*spans[part]))
-        return pltpu.make_async_remote_copy(
-            src_ref=stats.at[pick],
-            dst_ref=peers.at[(j - 1,) + pick],
-            send_sem=stat_send.at[part, j - 1],
-            recv_sem=stat_recv.at[part, j - 1],
-            device_id={"lon": lax.rem(lon + j, lons)},
-            device_id_type=MESH,
-        )
-
-    pl.when(early == 1)(lambda: face(1).start())
-    for k in range(2, end + 1):
-        face(k).start()
+        return remote(stats.at[pick], peers.at[(j - 1,) + pick],
+                      stat_send.at[part, j - 1], stat_recv.at[part, j - 1],
+                      {"lon": lax.rem(lon + j, lons)})
+
+    def each_stat(part, act):
+        for j in range(1, lons):
+            act(stat(part, j))
+
+    @pl.when(early)
+    def _():
+        for k in range(1, end + 1):
+            face(k).start()
+
+    @pl.when(late)
+    def _():
+        for k in range(2, end if twin else end + 1):
+            face(k).start()
+        if twin:
+            for i in (1, 0, 2):
+                tile_copy(i).start()
+
     for j in range(1, lons):
         there = lax.rem(lon + j, lons)
-        ahead = (1 - lax.rem(there, 2)) * lons + there < order
-        pl.when(ahead)(lambda: signal(entered, {"lon": there}))
+        pl.when(ahead(there))(lambda: signal(entered, {"lon": there}))
 
     def finish(at, add):
         values = [edge[c, pl.ds(at, 8)] for c in range(cols)]
@@ -461,64 +486,116 @@
         for c in range(cols):
             out_scaled[c, pl.ds(at, 8)] = (out_dens[c, pl.ds(at, 8)] - mean) * gain
 
+    def land(k):
+        face(k).wait_recv()
+        tiles(*fine[k], lambda at: finish(at, True))
+
     tiles(*fine[0], lambda at: finish(at, False))
-    for k in range(1, end + 1):
-        if k == 1:
-            pl.when(early == 0)(lambda: tiles(*fine[k], lambda at: finish(at, False)))
-
-            @pl.when(early == 1)
-            def _():
-                face(k).wait_recv()
-                tiles(*fine[k], lambda at: finish(at, True))
-        else:
-            face(k).wait_recv()
-            tiles(*fine[k], lambda at: finish(at, True))
-        if k == 1:
-            pl.when(before < lons - 1)(lambda: pl.semaphore_wait(entered, lons - 1 - before))
-        for j in range(1, lons):
-            stat(k - 1, j).start()
-        if k > 1:
-            for j in range(1, lons):
-                stat(k - 2, j).wait_recv()
-            tiles(*spans[k - 2], scale)
-    pl.when(early == 1)(lambda: face(1).wait_send())
-    for k in range(2, end + 1):
-        face(k).wait_send()
-    for j in range(1, lons):
-        stat(end - 1, j).wait_recv()
-    tiles(*spans[end - 1], scale)
-    for part in range(len(spans)):
-        for j in range(1, lons):
-            stat(part, j).wait_send()
-
-
-def write_last(scaled, dens, in_scaled, in_dens, out_scaled, out_dens, sems):
-    del in_scaled, in_dens
+    pl.when(late)(lambda: tiles(*fine[1], lambda at: finish(at, False)))
+    pl.when(early)(lambda: land(1))
+    pl.when(before < lons - 1)(lambda: pl.semaphore_wait(entered, lons - 1 - before))
+    each_stat(0, lambda copy: copy.start())
+    land(2)
+    each_stat(1, lambda copy: copy.start())
+    each_stat(0, lambda copy: copy.wait_recv())
+    tiles(*spans[0], scale)
+    if twin:
+        @pl.when(early)
+        def _():
+            land(end)
+            tile_copy(3).start()
+            tile_sums[...] = stats[:, tail]
+    else:
+        land(end)
+        each_stat(2, lambda copy: copy.start())
+    each_stat(1, lambda copy: copy.wait_recv())
+    tiles(*spans[1], scale)
+
+    face(2).wait_send()
+    for part in range(2):
+        each_stat(part, lambda copy: copy.wait_send())
+    if twin:
+        @pl.when(early)
+        def _():
+            face(1).wait_send()
+            face(end).wait_send()
+            tile_copy(3).wait_send()
+            tile_copy(2).wait_recv()
+            tile_copy(1).wait_recv()
+
+        @pl.when(late)
+        def _():
+            tile_base[...] = edge[:, tail]
+            for i in range(3):
+                tile_copy(i).wait_send()
+            tile_copy(3).wait_recv()
+            tile_copy(0).wait_recv()
+    else:
+        pl.when(early)(lambda: face(1).wait_send())
+        face(end).wait_send()
+        each_stat(2, lambda copy: copy.wait_recv())
+        tiles(*spans[2], scale)
+        each_stat(2, lambda copy: copy.wait_send())
+
+
+def write_last(lons, scaled, dens, *refs):
+    twin = lons == 2
+    if twin:
+        tile_base, tile_face, tile_sums, _, _, out_scaled, out_dens, sems = refs[:8]
+        own_scaled, own_dens, tile_sem = refs[8:]
+    else:
+        _, _, out_scaled, out_dens, sems = refs
     rows, many = out_dens.shape[0], sems.shape[1]
     cols, deep, _ = dens.shape
     _, _, fine = split(deep)
-    late = lax.rem(lax.axis_index("lon"), 2) == 0
-
-    def copies(src, dst, i, known):
-        step = cols // many
+    last = fine[-1][0]
+    late = lax.rem(lax.axis_index("lon"), 2)
+
+    def copies(src, dst, i, begin, end):
+        step, span = cols // many, pl.ds(begin, end - begin)
         return [
             pltpu.make_async_copy(
-                src.at[pl.ds(part * step, step), pl.ds(known, deep - known)],
-                dst.at[place(1, rows), pl.ds(part * step, step), pl.ds(known, deep - known)],
+                src.at[pl.ds(part * step, step), span],
+                dst.at[place(1, rows), pl.ds(part * step, step), span],
                 sems.at[i, part])
             for part in range(many)
         ]
 
     def each(act):
-        for copy in copies(scaled, out_scaled, 0, 0):
+        for copy in copies(scaled, out_scaled, 0, 0, last if twin else deep):
             act(copy)
         for moved in range(2):
             @pl.when(late == moved)
             def _():
-                for copy in copies(dens, out_dens, 1, sum(fine[moved])):
+                stop = last if twin and moved else deep
+                for copy in copies(dens, out_dens, 1, sum(fine[moved]), stop):
                     act(copy)
 
+    def tile_out(i):
+        src, dst = ((own_scaled, out_scaled), (own_dens, out_dens))[i]
+        return pltpu.make_async_copy(
+            src, dst.at[place(1, rows), :, pl.ds(last, 8)], tile_sem.at[i])
+
     each(lambda copy: copy.start())
+    if twin:
+        values = [tile_base[c] + 0.1 * tile_face[c] for c in range(cols)]
+        mean, gain = line_scale([line_sums(values), (tile_sums[0], tile_sums[1])], cols)
+
+        @pl.when(late == 1)
+        def _():
+            for c in range(cols):
+                own_dens[c] = values[c]
+                own_scaled[c] = (values[c] - mean) * gain
+            tile_out(1).start()
+
+        @pl.when(late == 0)
+        def _():
+            for c in range(cols):
+                own_scaled[c] = (dens[c, pl.ds(last, 8)] - mean) * gain
+
+        tile_out(0).start()
+        pl.when(late == 1)(lambda: tile_out(1).wait())
+        tile_out(0).wait()
     each(lambda copy: copy.wait())
 
 
@@ -571,11 +648,14 @@
         compiler_params=pltpu.CompilerParams(vmem_limit_bytes=2**20),
     )(*in_vmem(scaled, dens, edge))
 
-    row_scaled, row_dens = pl.pallas_call(
+    twin = lons == 2
+    tile = pltpu.VMEM((cols, 8, lanes), jnp.float32)
+    extra = (tile, tile, pltpu.VMEM((2, 8, lanes), jnp.float32)) if twin else ()
+    row_parts = pl.pallas_call(
         functools.partial(last_row, lons),
-        out_shape=(row, row),
+        out_shape=(row, row) + extra,
         in_specs=[vmem] * 3,
-        out_specs=[vmem] * 2,
+        out_specs=[vmem] * (2 + len(extra)),
         scratch_shapes=[
             pltpu.VMEM((cols, deep, lanes), jnp.float32),
             pltpu.VMEM((2, deep, lanes), jnp.float32),
@@ -585,6 +665,8 @@
             sem((len(fine),)),
             sem((len(fine) - 1, peers)),
             sem((len(fine) - 1, peers)),
+            sem((4,)),
+            sem((4,)),
         ],
         compiler_params=pltpu.CompilerParams(
             collective_id=1, has_side_effects=True, vmem_limit_bytes=8 * 2**20
@@ -592,15 +674,16 @@
     )(*in_vmem(edge, front, token))
 
     hbm = pl.BlockSpec(memory_space=pltpu.HBM)
+    known = len(row_parts)
     return pl.pallas_call(
-        write_last,
+        functools.partial(write_last, lons),
         out_shape=(out, out),
-        in_specs=[vmem] * 2 + [hbm] * 2,
+        in_specs=[vmem] * known + [hbm] * 2,
         out_specs=[hbm] * 2,
-        input_output_aliases={2: 0, 3: 1},
-        scratch_shapes=[sem((2, 4 if cols % 4 == 0 else 1))],
+        input_output_aliases={known: 0, known + 1: 1},
+        scratch_shapes=[sem((2, 4 if cols % 4 == 0 else 1))] + ([tile, tile, sem((2,))] if twin else []),
         compiler_params=pltpu.CompilerParams(vmem_limit_bytes=2**20),
-    )(*in_vmem(row_scaled, row_dens), out_scaled, out_dens)
+    )(*in_vmem(*row_parts), out_scaled, out_dens)
 
 
 VMEM_LIMIT = 44 * 2**20

time: 97.8 us -> 101 us (1.033)
  Pallas kernels: 97 us -> 100 us
    pallas_call x1, Pallas kernels: 77.6 us -> 84.8 us  [all_steps(): pl.pallas_call(functools.partial(kernel, lons, levs), out_shape=(inner, i...]
    pallas_call x2, Pallas kernels: 16.4 us -> 12.4 us  [the longest x1 11.2 us: all_steps(): pl.pallas_call(functools.partial(last_row, lons), out_shape=(row, row) +...]
where the time goes in v5:
time: 101 us
  Pallas kernels  100 us (99%)
    pallas_call x1, Pallas kernels, all_steps(): pl.pallas_call(functools.partial(kernel, lons, levs), out_shape=(inner, i...  84.8 us
    pallas_call x1, Pallas kernels, all_steps(): pl.pallas_call(functools.partial(last_row, lons), out_shape=(row, row) +...  11.2 us
    pallas_call x1, Pallas kernels, all_steps(): pl.pallas_call(write_inner, out_shape=(out, out, pltpu.VMEM((8, lanes), j...  3.06 us

profile of v5, /device:TPU:1, one launch (start us, length us, event | category | flops | bytes accessed | tf_op | source)
XLA Modules:
  0.0 100.8 jit_solution(10019160263180038862)
XLA Ops:
  0.6 84.8 %shard_map.41 = (f32[3,16,128,128]{3,2,1,0:T(8,128)S(1)}, f32[3,16,128,128]{3,2,1,0:T(8,128)S(1)}, f32[16,128,128]{2,1,0:T(8,128)S(1)}, f32[16,128,128]{2,1,0:T(8,128)S(1)}) custom-call(f32[4,16,128,128]{3,2,1,0:T(8,128)} %dens.1, f32[4,16,128,128]{3,2,1,0:T(8,128)} %crowd.1), custom_call_target="tpu_custom_call" | custom-call | tf_op jit(solution)/shard_map/pallas_call | solution.py:615
  85.4 3.1 %shard_map.42 = (f32[4,16,128,128]{3,2,1,0:T(8,128)}, f32[4,16,128,128]{3,2,1,0:T(8,128)}, f32[8,128]{1,0:T(8,128)S(1)}) custom-call(f32[3,16,128,128]{3,2,1,0:T(8,128)S(1)} %get-tuple-element.16.scaled, f32[3,16,128,128]{3,2,1,0:T(8,128)S(1)} %get-tuple-element.17.dens, f32[16,128,128]{2,1,0:T(8,128)S(1)} %get-tuple-element.14.edge), custom_call_target="tpu_custom_call" | custom-call | tf_op jit(solution)/shard_map/pallas_call | solution.py:642
  88.5 11.2 %shard_map.43 = (f32[16,128,128]{2,1,0:T(8,128)S(1)}, f32[16,128,128]{2,1,0:T(8,128)S(1)}, f32[16,8,128]{2,1,0:T(8,128)S(1)}, f32[16,8,128]{2,1,0:T(8,128)S(1)}, f32[2,8,128]{2,1,0:T(8,128)S(1)}) custom-call(f32[16,128,128]{2,1,0:T(8,128)S(1)} %get-tuple-element.14.edge, f32[16,128,128]{2,1,0:T(8,128)S(1)} %get-tuple-element.15.front, ...), custom_call_target="tpu_custom_call" | custom-call | tf_op jit(solution)/shard_map/pallas_call | solution.py:654
  99.7 1.1 %shard_map.44 = (f32[4,16,128,128]{3,2,1,0:T(8,128)}, f32[4,16,128,128]{3,2,1,0:T(8,128)}) custom-call(f32[16,128,128]{2,1,0:T(8,128)S(1)} %get-tuple-element.19.scaled, f32[16,128,128]{2,1,0:T(8,128)S(1)} %get-tuple-element.20.dens, f32[16,8,128]{2,1,0:T(8,128)S(1)} %get-tuple-element.21.refs_0_, ...), custom_call_target="tpu_custom_call", output_to_operand_aliasing={{0}: (5, {}), {1}: (6, {})} | custom-call | tf_op jit(solution)/shard_map/pallas_call | solution.py:678

commit v6 on v5

--- a/solution.py
+++ b/solution.py
@@ -119,7 +119,7 @@
     lat, lon, lev = lax.axis_index("lat"), lax.axis_index("lon"), lax.axis_index("lev")
     has_left, has_right = lon > 0, lon < lons - 1
     has_down, has_up = lev > 0, lev < levs - 1
-    late = lax.rem(lon, 2) == 1
+    late = lax.rem(lon, 2) == 0
 
     first = [
         pltpu.make_async_copy(
@@ -403,11 +403,11 @@
     spans = [(0, sum(fine[1]))] + fine[2:]
     tail = pl.ds(*fine[end])
     lat, lon = lax.axis_index("lat"), lax.axis_index("lon")
-    late = lax.rem(lon, 2) == 1
+    late = lax.rem(lon, 2) == 0
     early = jnp.logical_not(late)
 
     def ahead(there):
-        return lax.rem(there, 2) * lons + there < lax.rem(lon, 2) * lons + lon
+        return there - lax.rem(there, 2) * lons < lon - lax.rem(lon, 2) * lons
 
     barrier = pltpu.get_barrier_semaphore()
     signal(barrier, {"lat": 1 - lat})
@@ -549,7 +549,7 @@
     cols, deep, _ = dens.shape
     _, _, fine = split(deep)
     last = fine[-1][0]
-    late = lax.rem(lax.axis_index("lon"), 2)
+    late = 1 - lax.rem(lax.axis_index("lon"), 2)
 
     def copies(src, dst, i, begin, end):
         step, span = cols // many, pl.ds(begin, end - begin)

time: 101 us -> 97.7 us (0.967)
  Pallas kernels: 100 us -> 96.5 us
    pallas_call x1, Pallas kernels: 84.8 us -> 77.6 us  [all_steps(): pl.pallas_call(functools.partial(kernel, lons, levs), out_shape=(inner, i...]
    pallas_call x1, Pallas kernels: 11.2 us -> 14.5 us  [all_steps(): pl.pallas_call(functools.partial(last_row, lons), out_shape=(row, row) +...]
where the time goes in v6:
time: 97.7 us; the launch traced here: 97.1 us
  Pallas kernels  96.5 us (99%)
    pallas_call x1, Pallas kernels, all_steps(): pl.pallas_call(functools.partial(kernel, lons, levs), out_shape=(inner, i...  77.6 us
    pallas_call x1, Pallas kernels, all_steps(): pl.pallas_call(functools.partial(last_row, lons), out_shape=(row, row) +...  14.5 us
    pallas_call x1, Pallas kernels, all_steps(): pl.pallas_call(write_inner, out_shape=(out, out, pltpu.VMEM((8, lanes), j...  3.06 us

profile of v6, /device:TPU:1, one launch (start us, length us, event | category | flops | bytes accessed | tf_op | source)
XLA Modules:
  0.0 97.1 jit_solution(5007406413619487203)
XLA Ops:
  0.6 77.6 %shard_map.41 = (f32[3,16,128,128]{3,2,1,0:T(8,128)S(1)}, f32[3,16,128,128]{3,2,1,0:T(8,128)S(1)}, f32[16,128,128]{2,1,0:T(8,128)S(1)}, f32[16,128,128]{2,1,0:T(8,128)S(1)}) custom-call(f32[4,16,128,128]{3,2,1,0:T(8,128)} %dens.1, f32[4,16,128,128]{3,2,1,0:T(8,128)} %crowd.1), custom_call_target="tpu_custom_call" | custom-call | tf_op jit(solution)/shard_map/pallas_call | solution.py:615
  78.2 3.1 %shard_map.42 = (f32[4,16,128,128]{3,2,1,0:T(8,128)}, f32[4,16,128,128]{3,2,1,0:T(8,128)}, f32[8,128]{1,0:T(8,128)S(1)}) custom-call(f32[3,16,128,128]{3,2,1,0:T(8,128)S(1)} %get-tuple-element.16.scaled, f32[3,16,128,128]{3,2,1,0:T(8,128)S(1)} %get-tuple-element.17.dens, f32[16,128,128]{2,1,0:T(8,128)S(1)} %get-tuple-element.14.edge), custom_call_target="tpu_custom_call" | custom-call | tf_op jit(solution)/shard_map/pallas_call | solution.py:642
  81.3 14.5 %shard_map.43 = (f32[16,128,128]{2,1,0:T(8,128)S(1)}, f32[16,128,128]{2,1,0:T(8,128)S(1)}, f32[16,8,128]{2,1,0:T(8,128)S(1)}, f32[16,8,128]{2,1,0:T(8,128)S(1)}, f32[2,8,128]{2,1,0:T(8,128)S(1)}) custom-call(f32[16,128,128]{2,1,0:T(8,128)S(1)} %get-tuple-element.14.edge, f32[16,128,128]{2,1,0:T(8,128)S(1)} %get-tuple-element.15.front, ...), custom_call_target="tpu_custom_call" | custom-call | tf_op jit(solution)/shard_map/pallas_call | solution.py:654
  95.8 1.3 %shard_map.44 = (f32[4,16,128,128]{3,2,1,0:T(8,128)}, f32[4,16,128,128]{3,2,1,0:T(8,128)}) custom-call(f32[16,128,128]{2,1,0:T(8,128)S(1)} %get-tuple-element.19.scaled, f32[16,128,128]{2,1,0:T(8,128)S(1)} %get-tuple-element.20.dens, f32[16,8,128]{2,1,0:T(8,128)S(1)} %get-tuple-element.21.refs_0_, ...), custom_call_target="tpu_custom_call", output_to_operand_aliasing={{0}: (5, {}), {1}: (6, {})} | custom-call | tf_op jit(solution)/shard_map/pallas_call | solution.py:678

commit v7 on v6

--- a/solution.py
+++ b/solution.py
@@ -97,6 +97,10 @@
     lax.fori_loop(first // 8, (first + many) // 8, tile, 0)
 
 
+def ahead(there, lon, lons):
+    return there - lax.rem(there, 2) * lons < lon - lax.rem(lon, 2) * lons
+
+
 def line_sums(values):
     cols = len(values)
     total = tree_sum(values)
@@ -112,7 +116,7 @@
 
 
 def kernel(lons, levs, dens, crowd, out_scaled, out_dens, edge, front,
-           field, cap, stats, peers, load_sem, edge_sem, face_send, face_recv,
+           field, cap, stats, peers, entered, load_sem, edge_sem, face_send, face_recv,
            lon_send, lon_recv, lev_send, lev_recv, stat_send, stat_recv):
     rows, cols, deep, lanes = dens.shape
     opening, coarse, fine = split(deep)
@@ -140,14 +144,28 @@
 
     barrier = pltpu.get_barrier_semaphore()
     signal(barrier, {"lat": 1 - lat})
+    before = 0
     for j in range(1, lons):
-        signal(barrier, {"lon": lax.rem(lon + j, lons)})
+        there = lax.rem(lon + j, lons)
+        before += ahead(there, lon, lons).astype(jnp.int32)
+        pl.when(jnp.logical_not(ahead(there, lon, lons)))(lambda: signal(barrier, {"lon": there}))
     if levs > 1:
-        pl.when(has_down)(lambda: signal(barrier, {"lev": lev - 1}))
         pl.when(has_up)(lambda: signal(barrier, {"lev": lev + 1}))
     for copy in first + loads:
         copy.start()
-    pl.semaphore_wait(barrier, lons + has_down.astype(jnp.int32) + has_up.astype(jnp.int32))
+    pl.semaphore_wait(barrier, 1 + before + has_down.astype(jnp.int32))
+
+    def greet():
+        for j in range(1, lons):
+            there = lax.rem(lon + j, lons)
+            pl.when(ahead(there, lon, lons))(lambda: signal(entered.at[0], {"lon": there}))
+        if levs > 1:
+            pl.when(has_down)(lambda: signal(entered.at[1], {"lev": lev - 1}))
+
+    def wait_greeted():
+        pl.when(before < lons - 1)(lambda: pl.semaphore_wait(entered.at[0], lons - 1 - before))
+        if levs > 1:
+            pl.when(has_up)(lambda: pl.semaphore_wait(entered.at[1], 1))
 
     def chunks(t):
         return opening if t == 0 else fine if t == STEPS - 1 else coarse
@@ -227,6 +245,8 @@
     for k in range(len(opening)):
         first[k].wait()
         face(0, k).start()
+        if k == 0:
+            greet()
 
     def clear_cols(at):
         for t in range(STEPS):
@@ -251,6 +271,7 @@
 
     for copy in loads:
         copy.wait()
+    wait_greeted()
     start_sides(0, 1)
     start_sides(0, 0)
 
@@ -406,17 +427,14 @@
     late = lax.rem(lon, 2) == 0
     early = jnp.logical_not(late)
 
-    def ahead(there):
-        return there - lax.rem(there, 2) * lons < lon - lax.rem(lon, 2) * lons
-
     barrier = pltpu.get_barrier_semaphore()
     signal(barrier, {"lat": 1 - lat})
     before = 0
     for j in range(1, lons):
         there = lax.rem(lon + j, lons)
-        before += ahead(there).astype(jnp.int32)
-
-        @pl.when(jnp.logical_not(ahead(there)))
+        before += ahead(there, lon, lons).astype(jnp.int32)
+
+        @pl.when(jnp.logical_not(ahead(there, lon, lons)))
         def _():
             signal(barrier, {"lon": there})
             if twin:
@@ -466,7 +484,7 @@
 
     for j in range(1, lons):
         there = lax.rem(lon + j, lons)
-        pl.when(ahead(there))(lambda: signal(entered, {"lon": there}))
+        pl.when(ahead(there, lon, lons))(lambda: signal(entered, {"lon": there}))
 
     def finish(at, add):
         values = [edge[c, pl.ds(at, 8)] for c in range(cols)]
@@ -622,6 +640,7 @@
             pltpu.VMEM((rows, cols, deep, lanes), jnp.float32),
             pltpu.VMEM((rows - 1, 2, deep, lanes), jnp.float32),
             pltpu.VMEM((peers, rows - 1, 2, deep, lanes), jnp.float32),
+            pltpu.SemaphoreType.REGULAR((2,)),
             sem((2, rows)),
             sem((len(opening),)),
             sem((STEPS, len(fine))),

time: 97.7 us -> 97.3 us (level)
  no operation moved by 1% of the time
where the time goes in v7:
time: 97.3 us; the launch traced here: 96.7 us
  Pallas kernels  96.1 us (99%)
    pallas_call x1, Pallas kernels, all_steps(): pl.pallas_call(functools.partial(kernel, lons, levs), out_shape=(inner, i...  77.5 us
    pallas_call x1, Pallas kernels, all_steps(): pl.pallas_call(functools.partial(last_row, lons), out_shape=(row, row) +...  14.2 us
    pallas_call x1, Pallas kernels, all_steps(): pl.pallas_call(write_inner, out_shape=(out, out, pltpu.VMEM((8, lanes), j...  3.06 us

profile of v7, /device:TPU:1, one launch (start us, length us, event | category | flops | bytes accessed | tf_op | source)
XLA Modules:
  0.0 96.7 jit_solution(11909455342212597221)
XLA Ops:
  0.6 77.5 %shard_map.41 = (f32[3,16,128,128]{3,2,1,0:T(8,128)S(1)}, f32[3,16,128,128]{3,2,1,0:T(8,128)S(1)}, f32[16,128,128]{2,1,0:T(8,128)S(1)}, f32[16,128,128]{2,1,0:T(8,128)S(1)}) custom-call(f32[4,16,128,128]{3,2,1,0:T(8,128)} %dens.1, f32[4,16,128,128]{3,2,1,0:T(8,128)} %crowd.1), custom_call_target="tpu_custom_call" | custom-call | tf_op jit(solution)/shard_map/pallas_call | solution.py:633
  78.1 3.1 %shard_map.42 = (f32[4,16,128,128]{3,2,1,0:T(8,128)}, f32[4,16,128,128]{3,2,1,0:T(8,128)}, f32[8,128]{1,0:T(8,128)S(1)}) custom-call(f32[3,16,128,128]{3,2,1,0:T(8,128)S(1)} %get-tuple-element.16.scaled, f32[3,16,128,128]{3,2,1,0:T(8,128)S(1)} %get-tuple-element.17.dens, f32[16,128,128]{2,1,0:T(8,128)S(1)} %get-tuple-element.14.edge), custom_call_target="tpu_custom_call" | custom-call | tf_op jit(solution)/shard_map/pallas_call | solution.py:661
  81.2 14.2 %shard_map.43 = (f32[16,128,128]{2,1,0:T(8,128)S(1)}, f32[16,128,128]{2,1,0:T(8,128)S(1)}, f32[16,8,128]{2,1,0:T(8,128)S(1)}, f32[16,8,128]{2,1,0:T(8,128)S(1)}, f32[2,8,128]{2,1,0:T(8,128)S(1)}) custom-call(f32[16,128,128]{2,1,0:T(8,128)S(1)} %get-tuple-element.14.edge, f32[16,128,128]{2,1,0:T(8,128)S(1)} %get-tuple-element.15.front, ...), custom_call_target="tpu_custom_call" | custom-call | tf_op jit(solution)/shard_map/pallas_call | solution.py:673
  95.4 1.3 %shard_map.44 = (f32[4,16,128,128]{3,2,1,0:T(8,128)}, f32[4,16,128,128]{3,2,1,0:T(8,128)}) custom-call(f32[16,128,128]{2,1,0:T(8,128)S(1)} %get-tuple-element.19.scaled, f32[16,128,128]{2,1,0:T(8,128)S(1)} %get-tuple-element.20.dens, f32[16,8,128]{2,1,0:T(8,128)S(1)} %get-tuple-element.21.refs_0_, ...), custom_call_target="tpu_custom_call", output_to_operand_aliasing={{0}: (5, {}), {1}: (6, {})} | custom-call | tf_op jit(solution)/shard_map/pallas_call | solution.py:697

commit v8 on v7

--- a/solution.py
+++ b/solution.py
@@ -479,7 +479,7 @@
         for k in range(2, end if twin else end + 1):
             face(k).start()
         if twin:
-            for i in (1, 0, 2):
+            for i in (2, 0, 1):
                 tile_copy(i).start()
 
     for j in range(1, lons):

time: 97.3 us -> 96.9 us (level)
  no operation moved by 1% of the time
where the time goes in v8:
time: 96.9 us; the launch traced here: 96.7 us
  Pallas kernels  96.1 us (99%)
    pallas_call x1, Pallas kernels, all_steps(): pl.pallas_call(functools.partial(kernel, lons, levs), out_shape=(inner, i...  77.5 us
    pallas_call x1, Pallas kernels, all_steps(): pl.pallas_call(functools.partial(last_row, lons), out_shape=(row, row) +...  14.2 us
    pallas_call x1, Pallas kernels, all_steps(): pl.pallas_call(write_inner, out_shape=(out, out, pltpu.VMEM((8, lanes), j...  3.06 us

profile of v8, /device:TPU:1, one launch (start us, length us, event | category | flops | bytes accessed | tf_op | source)
XLA Modules:
  0.0 96.7 jit_solution(8802867257604208305)
XLA Ops:
  0.6 77.5 %shard_map.41 = (f32[3,16,128,128]{3,2,1,0:T(8,128)S(1)}, f32[3,16,128,128]{3,2,1,0:T(8,128)S(1)}, f32[16,128,128]{2,1,0:T(8,128)S(1)}, f32[16,128,128]{2,1,0:T(8,128)S(1)}) custom-call(f32[4,16,128,128]{3,2,1,0:T(8,128)} %dens.1, f32[4,16,128,128]{3,2,1,0:T(8,128)} %crowd.1), custom_call_target="tpu_custom_call" | custom-call | tf_op jit(solution)/shard_map/pallas_call | solution.py:633
  78.1 3.1 %shard_map.42 = (f32[4,16,128,128]{3,2,1,0:T(8,128)}, f32[4,16,128,128]{3,2,1,0:T(8,128)}, f32[8,128]{1,0:T(8,128)S(1)}) custom-call(f32[3,16,128,128]{3,2,1,0:T(8,128)S(1)} %get-tuple-element.16.scaled, f32[3,16,128,128]{3,2,1,0:T(8,128)S(1)} %get-tuple-element.17.dens, f32[16,128,128]{2,1,0:T(8,128)S(1)} %get-tuple-element.14.edge), custom_call_target="tpu_custom_call" | custom-call | tf_op jit(solution)/shard_map/pallas_call | solution.py:661
  81.2 14.2 %shard_map.43 = (f32[16,128,128]{2,1,0:T(8,128)S(1)}, f32[16,128,128]{2,1,0:T(8,128)S(1)}, f32[16,8,128]{2,1,0:T(8,128)S(1)}, f32[16,8,128]{2,1,0:T(8,128)S(1)}, f32[2,8,128]{2,1,0:T(8,128)S(1)}) custom-call(f32[16,128,128]{2,1,0:T(8,128)S(1)} %get-tuple-element.14.edge, f32[16,128,128]{2,1,0:T(8,128)S(1)} %get-tuple-element.15.front, ...), custom_call_target="tpu_custom_call" | custom-call | tf_op jit(solution)/shard_map/pallas_call | solution.py:673
  95.4 1.3 %shard_map.44 = (f32[4,16,128,128]{3,2,1,0:T(8,128)}, f32[4,16,128,128]{3,2,1,0:T(8,128)}) custom-call(f32[16,128,128]{2,1,0:T(8,128)S(1)} %get-tuple-element.19.scaled, f32[16,128,128]{2,1,0:T(8,128)S(1)} %get-tuple-element.20.dens, f32[16,8,128]{2,1,0:T(8,128)S(1)} %get-tuple-element.21.refs_0_, ...), custom_call_target="tpu_custom_call", output_to_operand_aliasing={{0}: (5, {}), {1}: (6, {})} | custom-call | tf_op jit(solution)/shard_map/pallas_call | solution.py:697

commit v9 on v8

--- a/solution.py
+++ b/solution.py
@@ -132,15 +132,17 @@
             edge_sem.at[k])
         for k, (at, span) in enumerate(opening)
     ]
-    loads = []
-    for r in range(1, rows + 1):
-        if r > 1:
-            loads.append(pltpu.make_async_copy(
-                dens.at[place(r, rows)],
-                field.at[0, r, pl.ds(1, cols), pl.ds(PAD, deep)],
-                load_sem.at[0, r - 1]))
-        loads.append(pltpu.make_async_copy(
-            crowd.at[place(r, rows)], cap.at[r - 1], load_sem.at[1, r - 1]))
+    loads = [pltpu.make_async_copy(crowd, cap, load_sem.at[0])] + [
+        pltpu.make_async_copy(
+            dens.at[place(r, rows)],
+            field.at[0, r, pl.ds(1, cols), pl.ds(PAD, deep)],
+            load_sem.at[1])
+        for r in range(2, rows + 1)
+    ]
+    all_rows = pltpu.make_async_copy(
+        dens.at[pl.ds(0, rows - 1)],
+        field.at[0, pl.ds(2, rows - 1), pl.ds(1, cols), pl.ds(PAD, deep)],
+        load_sem.at[1])
 
     barrier = pltpu.get_barrier_semaphore()
     signal(barrier, {"lat": 1 - lat})
@@ -175,13 +177,17 @@
         return pltpu.make_async_remote_copy(
             src_ref=field.at[t, 1, pl.ds(1, cols), pl.ds(PAD + at, span)],
             dst_ref=field.at[t, 0, pl.ds(1, cols), pl.ds(PAD + at, span)],
-            send_sem=face_send.at[t, k],
-            recv_sem=face_recv.at[t, k],
+            send_sem=face_send.at[k],
+            recv_sem=face_recv.at[t % 2, k],
             device_id={"lat": 1 - lat},
             device_id_type=MESH,
         )
 
     bands = (pl.ds(1, 1), pl.ds(2, rows - 1))
+    sent = []
+
+    def way(count, forward):
+        return int(forward) if count > 2 else 0
 
     def lon_side(t, band, right):
         own, theirs = (cols, 0) if right else (1, cols + 1)
@@ -189,8 +195,8 @@
         return pltpu.make_async_remote_copy(
             src_ref=field.at[t, span, own, pl.ds(PAD, deep)],
             dst_ref=field.at[t, span, theirs, pl.ds(PAD, deep)],
-            send_sem=lon_send.at[t, band, int(right)],
-            recv_sem=lon_recv.at[t, band, int(right)],
+            send_sem=lon_send.at[way(lons, right)],
+            recv_sem=lon_recv.at[t % 2, band, way(lons, right)],
             device_id={"lon": lon + 1 if right else lon - 1},
             device_id_type=MESH,
         )
@@ -201,8 +207,8 @@
         return pltpu.make_async_remote_copy(
             src_ref=field.at[t, span[0], span[1], pl.ds(own, 1)],
             dst_ref=field.at[t, span[0], span[1], pl.ds(theirs, 1)],
-            send_sem=lev_send.at[t, band, int(up)],
-            recv_sem=lev_recv.at[t, band, int(up)],
+            send_sem=lev_send.at[way(levs, up)],
+            recv_sem=lev_recv.at[t % 2, band, way(levs, up)],
             device_id={"lev": lev + 1 if up else lev - 1},
             device_id_type=MESH,
         )
@@ -215,11 +221,14 @@
             pl.when(has_up)(lambda: act(lev_side(t, band, True)))
             pl.when(has_down)(lambda: act(lev_side(t, band, False)))
 
+    def wait_sides_sent():
+        if sent:
+            sides(*sent.pop(), lambda copy: copy.wait_send())
+
     def start_sides(t, band):
+        wait_sides_sent()
         sides(t, band, lambda copy: copy.start())
-
-    def wait_sides_sent(t, band):
-        sides(t, band, lambda copy: copy.wait_send())
+        sent.append((t, band))
 
     def wait_sides(t, band):
         if lons > 1:
@@ -230,13 +239,12 @@
             pl.when(has_up)(lambda: lev_side(t, band, False).wait_recv())
 
     stat_rows = (pl.ds(0, 1), pl.ds(1, rows - 2))
-    groups = range(2 if rows > 2 else 1)
 
     def stat(group, j):
         return pltpu.make_async_remote_copy(
             src_ref=stats.at[stat_rows[group]],
             dst_ref=peers.at[j - 1, stat_rows[group]],
-            send_sem=stat_send.at[group, j - 1],
+            send_sem=stat_send.at[j - 1],
             recv_sem=stat_recv.at[group, j - 1],
             device_id={"lon": lax.rem(lon + j, lons)},
             device_id_type=MESH,
@@ -269,8 +277,8 @@
     pl.when(jnp.logical_not(has_down))(lambda: clear_level(0))
     pl.when(jnp.logical_not(has_up))(lambda: clear_level(PAD + deep))
 
-    for copy in loads:
-        copy.wait()
+    loads[0].wait()
+    all_rows.wait()
     wait_greeted()
     start_sides(0, 1)
     start_sides(0, 0)
@@ -283,7 +291,7 @@
             near += field[t, r - 1, c, pl.ds(PAD + at, span)]
         if above:
             near += field[t, r + 1, c, pl.ds(PAD + at, span)]
-        limit = cap[r - 1, c - 1, pl.ds(at, span)]
+        limit = cap[place(r, rows), c - 1, pl.ds(at, span)]
         return here * (0.6 - 0.2 * (here * limit)) + 0.1 * near
 
     def advance_row(t, r, at, span, last):
@@ -296,10 +304,14 @@
         lax.fori_loop(1, cols + 1, col, 0)
 
     def start_face(t, k):
+        def go():
+            face(t - 1, k).wait_send()
+            face(t, k).start()
+
         if t < STEPS - 1 or k == 0:
-            face(t, k).start()
+            go()
         elif k == 1:
-            pl.when(late)(lambda: face(t, k).start())
+            pl.when(late)(go)
 
     def finish(r, at, last):
         values = [cell(STEPS - 1, r, c, at, 8, True, not last) for c in range(1, cols + 1)]
@@ -325,6 +337,8 @@
 
     def send_sums(group):
         for j in range(1, lons):
+            if group == 0 and rows > 2:
+                stat(1, j).wait_send()
             stat(group, j).start()
 
     def wait_sums(group):
@@ -380,15 +394,12 @@
             return 0
         lax.fori_loop(0, cols, col, 0)
 
-    for s in range(STEPS - 1):
-        for k in range(len(chunks(s))):
-            face(s, k).wait_send()
-    for s in range(STEPS):
-        for band in range(2):
-            wait_sides_sent(s, band)
-    for group in groups:
-        for j in range(1, lons):
-            stat(group, j).wait_send()
+    for k in range(2, len(opening)):
+        face(0, k).wait_send()
+    wait_sides_sent()
+    for j in range(1, lons):
+        stat(0, j).wait_send()
+    pl.when(jnp.logical_not(late))(lambda: face(t - 1, 1).wait_send())
     add_face(0)
     face(t, 0).wait_send()
 
@@ -400,16 +411,14 @@
 
 def write_inner(scaled, dens, edge, out_scaled, out_dens, token, sems):
     inner, cols, _, _ = scaled.shape
-    copies = []
+    waits = [pltpu.make_async_copy(edge, out_dens.at[place(1, inner + 1)], sems.at[2])]
+    waits[0].start()
     for i, (src, dst) in enumerate(((scaled, out_scaled), (dens, out_dens))):
         for r in range(inner):
-            copies.append(pltpu.make_async_copy(
-                src.at[r], dst.at[place(r + 2, inner + 1)], sems.at[i, r]))
-    copies.append(pltpu.make_async_copy(edge, out_dens.at[place(1, inner + 1)], sems.at[1, inner]))
-    for copy in copies:
-        copy.start()
+            pltpu.make_async_copy(src.at[r], dst.at[place(r + 2, inner + 1)], sems.at[i]).start()
+        waits.append(pltpu.make_async_copy(src, dst.at[pl.ds(0, inner)], sems.at[i]))
     token[...] = jnp.zeros(token.shape, jnp.float32)
-    for copy in copies:
+    for copy in waits:
         copy.wait()
 
 
@@ -448,8 +457,14 @@
 
     def face(k):
         pick = (slice(None), pl.ds(*fine[k]))
-        return remote(front.at[pick], other.at[pick], face_send.at[k], face_recv.at[k],
+        return remote(front.at[pick], other.at[pick], face_send.at[0], face_recv.at[k - 1],
                       {"lat": 1 - lat})
+
+    def wait_faces_sent(k, stop):
+        at = fine[k][0]
+        pick = (slice(None), pl.ds(at, sum(fine[stop]) - at))
+        remote(front.at[pick], other.at[pick], face_send.at[0], face_recv.at[k - 1],
+               {"lat": 1 - lat}).wait_send()
 
     def tile_copy(i):
         src = (front, front, edge, stats)[i].at[:, tail]
@@ -457,12 +472,12 @@
         where = {"lat": 1 - lat} if i < 2 else {}
         if i > 0:
             where["lon"] = 1 - lon
-        return remote(src, dst, tile_send.at[i], tile_recv.at[i], where)
+        return remote(src, dst, tile_send.at[i % 3], tile_recv.at[i // 2], where)
 
     def stat(part, j):
         pick = (slice(None), pl.ds(*spans[part]))
         return remote(stats.at[pick], peers.at[(j - 1,) + pick],
-                      stat_send.at[part, j - 1], stat_recv.at[part, j - 1],
+                      stat_send.at[j - 1], stat_recv.at[part, j - 1],
                       {"lon": lax.rem(lon + j, lons)})
 
     def each_stat(part, act):
@@ -514,6 +529,7 @@
     pl.when(before < lons - 1)(lambda: pl.semaphore_wait(entered, lons - 1 - before))
     each_stat(0, lambda copy: copy.start())
     land(2)
+    each_stat(0, lambda copy: copy.wait_send())
     each_stat(1, lambda copy: copy.start())
     each_stat(0, lambda copy: copy.wait_recv())
     tiles(*spans[0], scale)
@@ -525,18 +541,18 @@
             tile_sums[...] = stats[:, tail]
     else:
         land(end)
+        each_stat(1, lambda copy: copy.wait_send())
         each_stat(2, lambda copy: copy.start())
     each_stat(1, lambda copy: copy.wait_recv())
     tiles(*spans[1], scale)
 
-    face(2).wait_send()
-    for part in range(2):
-        each_stat(part, lambda copy: copy.wait_send())
+    pl.when(early)(lambda: wait_faces_sent(1, end))
+    pl.when(late)(lambda: wait_faces_sent(2, end - 1 if twin else end))
     if twin:
+        each_stat(1, lambda copy: copy.wait_send())
+
         @pl.when(early)
         def _():
-            face(1).wait_send()
-            face(end).wait_send()
             tile_copy(3).wait_send()
             tile_copy(2).wait_recv()
             tile_copy(1).wait_recv()
@@ -549,8 +565,6 @@
             tile_copy(3).wait_recv()
             tile_copy(0).wait_recv()
     else:
-        pl.when(early)(lambda: face(1).wait_send())
-        face(end).wait_send()
         each_stat(2, lambda copy: copy.wait_recv())
         tiles(*spans[2], scale)
         each_stat(2, lambda copy: copy.wait_send())
@@ -563,31 +577,24 @@
         own_scaled, own_dens, tile_sem = refs[8:]
     else:
         _, _, out_scaled, out_dens, sems = refs
-    rows, many = out_dens.shape[0], sems.shape[1]
+    rows = out_dens.shape[0]
     cols, deep, _ = dens.shape
     _, _, fine = split(deep)
     last = fine[-1][0]
     late = 1 - lax.rem(lax.axis_index("lon"), 2)
 
-    def copies(src, dst, i, begin, end):
-        step, span = cols // many, pl.ds(begin, end - begin)
-        return [
-            pltpu.make_async_copy(
-                src.at[pl.ds(part * step, step), span],
-                dst.at[place(1, rows), pl.ds(part * step, step), span],
-                sems.at[i, part])
-            for part in range(many)
-        ]
+    def copy(src, dst, i, begin, end):
+        span = pl.ds(begin, end - begin)
+        return pltpu.make_async_copy(
+            src.at[:, span], dst.at[place(1, rows), :, span], sems.at[i])
 
     def each(act):
-        for copy in copies(scaled, out_scaled, 0, 0, last if twin else deep):
-            act(copy)
+        act(copy(scaled, out_scaled, 0, 0, last if twin else deep))
         for moved in range(2):
             @pl.when(late == moved)
             def _():
                 stop = last if twin and moved else deep
-                for copy in copies(dens, out_dens, 1, sum(fine[moved]), stop):
-                    act(copy)
+                act(copy(dens, out_dens, 1, sum(fine[moved]), stop))
 
     def tile_out(i):
         src, dst = ((own_scaled, out_scaled), (own_dens, out_dens))[i]
@@ -641,15 +648,15 @@
             pltpu.VMEM((rows - 1, 2, deep, lanes), jnp.float32),
             pltpu.VMEM((peers, rows - 1, 2, deep, lanes), jnp.float32),
             pltpu.SemaphoreType.REGULAR((2,)),
-            sem((2, rows)),
+            sem((2,)),
             sem((len(opening),)),
-            sem((STEPS, len(fine))),
-            sem((STEPS, len(fine))),
-            sem((STEPS, 2, 2)),
-            sem((STEPS, 2, 2)),
-            sem((STEPS, 2, 2)),
-            sem((STEPS, 2, 2)),
-            sem((2, peers)),
+            sem((len(opening),)),
+            sem((2, len(opening))),
+            sem((2 if lons > 2 else 1,)),
+            sem((2, 2, 2 if lons > 2 else 1)),
+            sem((2 if levs > 2 else 1,)),
+            sem((2, 2, 2 if levs > 2 else 1)),
+            sem((peers,)),
             sem((2, peers)),
         ],
         compiler_params=pltpu.CompilerParams(
@@ -663,7 +670,7 @@
         out_shape=(out, out, pltpu.VMEM((8, lanes), jnp.float32)),
         in_specs=[vmem] * 3,
         out_specs=[pl.BlockSpec(memory_space=pltpu.HBM)] * 2 + [vmem],
-        scratch_shapes=[sem((2, rows))],
+        scratch_shapes=[sem((3,))],
         compiler_params=pltpu.CompilerParams(vmem_limit_bytes=2**20),
     )(*in_vmem(scaled, dens, edge))
 
@@ -680,12 +687,12 @@
             pltpu.VMEM((2, deep, lanes), jnp.float32),
             pltpu.VMEM((peers, 2, deep, lanes), jnp.float32),
             pltpu.SemaphoreType.REGULAR,
-            sem((len(fine),)),
-            sem((len(fine),)),
-            sem((len(fine) - 1, peers)),
-            sem((len(fine) - 1, peers)),
-            sem((4,)),
-            sem((4,)),
+            sem((1,)),
+            sem((len(fine) - 1,)),
+            sem((peers,)),
+            sem((2 if twin else 3, peers)),
+            sem((3,)),
+            sem((2,)),
         ],
         compiler_params=pltpu.CompilerParams(
             collective_id=1, has_side_effects=True, vmem_limit_bytes=8 * 2**20
@@ -700,7 +707,7 @@
         in_specs=[vmem] * known + [hbm] * 2,
         out_specs=[hbm] * 2,
         input_output_aliases={known: 0, known + 1: 1},
-        scratch_shapes=[sem((2, 4 if cols % 4 == 0 else 1))] + ([tile, tile, sem((2,))] if twin else []),
+        scratch_shapes=[sem((2,))] + ([tile, tile, sem((2,))] if twin else []),
         compiler_params=pltpu.CompilerParams(vmem_limit_bytes=2**20),
     )(*in_vmem(*row_parts), out_scaled, out_dens)
 

time: 96.9 us -> 96.7 us (level)
  no operation moved by 1% of the time
where the time goes in v9:
time: 96.7 us; the launch traced here: 96.6 us
  Pallas kernels  95.9 us (99%)
    pallas_call x1, Pallas kernels, all_steps(): pl.pallas_call(functools.partial(kernel, lons, levs), out_shape=(inner, i...  76.7 us
    pallas_call x1, Pallas kernels, all_steps(): pl.pallas_call(functools.partial(last_row, lons), out_shape=(row, row) +...  14.9 us
    pallas_call x1, Pallas kernels, all_steps(): pl.pallas_call(write_inner, out_shape=(out, out, pltpu.VMEM((8, lanes), j...  3.02 us

profile of v9, /device:TPU:1, one launch (start us, length us, event | category | flops | bytes accessed | tf_op | source)
XLA Modules:
  0.0 96.6 jit_solution(14444612814549575899)
XLA Ops:
  0.6 76.7 %shard_map.41 = (f32[3,16,128,128]{3,2,1,0:T(8,128)S(1)}, f32[3,16,128,128]{3,2,1,0:T(8,128)S(1)}, f32[16,128,128]{2,1,0:T(8,128)S(1)}, f32[16,128,128]{2,1,0:T(8,128)S(1)}) custom-call(f32[4,16,128,128]{3,2,1,0:T(8,128)} %dens.1, f32[4,16,128,128]{3,2,1,0:T(8,128)} %crowd.1), custom_call_target="tpu_custom_call" | custom-call | tf_op jit(solution)/shard_map/pallas_call | solution.py:640
  77.4 3.0 %shard_map.42 = (f32[4,16,128,128]{3,2,1,0:T(8,128)}, f32[4,16,128,128]{3,2,1,0:T(8,128)}, f32[8,128]{1,0:T(8,128)S(1)}) custom-call(f32[3,16,128,128]{3,2,1,0:T(8,128)S(1)} %get-tuple-element.16.scaled, f32[3,16,128,128]{3,2,1,0:T(8,128)S(1)} %get-tuple-element.17.dens, f32[16,128,128]{2,1,0:T(8,128)S(1)} %get-tuple-element.14.edge), custom_call_target="tpu_custom_call" | custom-call | tf_op jit(solution)/shard_map/pallas_call | solution.py:668
  80.4 14.9 %shard_map.43 = (f32[16,128,128]{2,1,0:T(8,128)S(1)}, f32[16,128,128]{2,1,0:T(8,128)S(1)}, f32[16,8,128]{2,1,0:T(8,128)S(1)}, f32[16,8,128]{2,1,0:T(8,128)S(1)}, f32[2,8,128]{2,1,0:T(8,128)S(1)}) custom-call(f32[16,128,128]{2,1,0:T(8,128)S(1)} %get-tuple-element.14.edge, f32[16,128,128]{2,1,0:T(8,128)S(1)} %get-tuple-element.15.front, ...), custom_call_target="tpu_custom_call" | custom-call | tf_op jit(solution)/shard_map/pallas_call | solution.py:680
  95.3 1.3 %shard_map.44 = (f32[4,16,128,128]{3,2,1,0:T(8,128)}, f32[4,16,128,128]{3,2,1,0:T(8,128)}) custom-call(f32[16,128,128]{2,1,0:T(8,128)S(1)} %get-tuple-element.19.scaled, f32[16,128,128]{2,1,0:T(8,128)S(1)} %get-tuple-element.20.dens, f32[16,8,128]{2,1,0:T(8,128)S(1)} %get-tuple-element.21.refs_0_, ...), custom_call_target="tpu_custom_call", output_to_operand_aliasing={{0}: (5, {}), {1}: (6, {})} | custom-call | tf_op jit(solution)/shard_map/pallas_call | solution.py:704

commit v10 on v9

--- a/solution.py
+++ b/solution.py
@@ -79,10 +79,9 @@
 def split(deep):
     half, last = deep // 2, deep - 8
     first, late = max(8, deep // 32 * 8), max(8, deep // 64 * 8)
-    opening = [(0, 8), (8, half - 8), (half, half)]
     coarse = [(0, half), (half, half)]
     fine = [(0, first), (first, last - late - first), (last - late, late), (last, 8)]
-    return opening, coarse, fine
+    return coarse, fine
 
 
 def place(r, rows):
@@ -116,33 +115,24 @@
 
 
 def kernel(lons, levs, dens, crowd, out_scaled, out_dens, edge, front,
-           field, cap, stats, peers, entered, load_sem, edge_sem, face_send, face_recv,
+           field, cap, stats, peers, entered, load_sem, face_send, face_recv,
            lon_send, lon_recv, lev_send, lev_recv, stat_send, stat_recv):
     rows, cols, deep, lanes = dens.shape
-    opening, coarse, fine = split(deep)
+    coarse, fine = split(deep)
     lat, lon, lev = lax.axis_index("lat"), lax.axis_index("lon"), lax.axis_index("lev")
     has_left, has_right = lon > 0, lon < lons - 1
     has_down, has_up = lev > 0, lev < levs - 1
     late = lax.rem(lon, 2) == 0
 
-    first = [
-        pltpu.make_async_copy(
-            dens.at[place(1, rows), :, pl.ds(at, span)],
-            field.at[0, 1, pl.ds(1, cols), pl.ds(PAD + at, span)],
-            edge_sem.at[k])
-        for k, (at, span) in enumerate(opening)
-    ]
     loads = [pltpu.make_async_copy(crowd, cap, load_sem.at[0])] + [
         pltpu.make_async_copy(
             dens.at[place(r, rows)],
             field.at[0, r, pl.ds(1, cols), pl.ds(PAD, deep)],
             load_sem.at[1])
-        for r in range(2, rows + 1)
+        for r in range(1, rows + 1)
     ]
     all_rows = pltpu.make_async_copy(
-        dens.at[pl.ds(0, rows - 1)],
-        field.at[0, pl.ds(2, rows - 1), pl.ds(1, cols), pl.ds(PAD, deep)],
-        load_sem.at[1])
+        dens, field.at[0, pl.ds(1, rows), pl.ds(1, cols), pl.ds(PAD, deep)], load_sem.at[1])
 
     barrier = pltpu.get_barrier_semaphore()
     signal(barrier, {"lat": 1 - lat})
@@ -153,7 +143,7 @@
         pl.when(jnp.logical_not(ahead(there, lon, lons)))(lambda: signal(barrier, {"lon": there}))
     if levs > 1:
         pl.when(has_up)(lambda: signal(barrier, {"lev": lev + 1}))
-    for copy in first + loads:
+    for copy in loads:
         copy.start()
     pl.semaphore_wait(barrier, 1 + before + has_down.astype(jnp.int32))
 
@@ -170,12 +160,15 @@
             pl.when(has_up)(lambda: pl.semaphore_wait(entered.at[1], 1))
 
     def chunks(t):
-        return opening if t == 0 else fine if t == STEPS - 1 else coarse
+        return fine if t == STEPS - 1 else coarse
 
     def face(t, k):
         at, span = chunks(t)[k]
+        src = field.at[t, 1, pl.ds(1, cols), pl.ds(PAD + at, span)]
+        if t == 0:
+            src = dens.at[place(1, rows), :, pl.ds(at, span)]
         return pltpu.make_async_remote_copy(
-            src_ref=field.at[t, 1, pl.ds(1, cols), pl.ds(PAD + at, span)],
+            src_ref=src,
             dst_ref=field.at[t, 0, pl.ds(1, cols), pl.ds(PAD + at, span)],
             send_sem=face_send.at[k],
             recv_sem=face_recv.at[t % 2, k],
@@ -250,11 +243,9 @@
             device_id_type=MESH,
         )
 
-    for k in range(len(opening)):
-        first[k].wait()
+    for k in range(len(coarse)):
         face(0, k).start()
-        if k == 0:
-            greet()
+    greet()
 
     def clear_cols(at):
         for t in range(STEPS):
@@ -394,8 +385,6 @@
             return 0
         lax.fori_loop(0, cols, col, 0)
 
-    for k in range(2, len(opening)):
-        face(0, k).wait_send()
     wait_sides_sent()
     for j in range(1, lons):
         stat(0, j).wait_send()
@@ -428,7 +417,7 @@
     (other, stats, peers, entered, face_send, face_recv, stat_send, stat_recv,
      tile_send, tile_recv) = refs[3:] if twin else refs
     cols, deep, lanes = edge.shape
-    _, _, fine = split(deep)
+    _, fine = split(deep)
     end = len(fine) - 1
     spans = [(0, sum(fine[1]))] + fine[2:]
     tail = pl.ds(*fine[end])
@@ -579,7 +568,7 @@
         _, _, out_scaled, out_dens, sems = refs
     rows = out_dens.shape[0]
     cols, deep, _ = dens.shape
-    _, _, fine = split(deep)
+    _, fine = split(deep)
     last = fine[-1][0]
     late = 1 - lax.rem(lax.axis_index("lon"), 2)
 
@@ -630,7 +619,7 @@
 
 def all_steps(lons, levs, density, crowding):
     rows, cols, deep, lanes = density.shape
-    opening, coarse, fine = split(deep)
+    coarse, fine = split(deep)
     sem = pltpu.SemaphoreType.DMA
     peers = max(lons - 1, 1)
     inner = pltpu.VMEM((rows - 1, cols, deep, lanes), jnp.float32)
@@ -649,9 +638,8 @@
             pltpu.VMEM((peers, rows - 1, 2, deep, lanes), jnp.float32),
             pltpu.SemaphoreType.REGULAR((2,)),
             sem((2,)),
-            sem((len(opening),)),
-            sem((len(opening),)),
-            sem((2, len(opening))),
+            sem((len(coarse),)),
+            sem((2, len(coarse))),
             sem((2 if lons > 2 else 1,)),
             sem((2, 2, 2 if lons > 2 else 1)),
             sem((2 if levs > 2 else 1,)),

time: 96.7 us -> 96.1 us (level)
  no operation moved by 1% of the time
where the time goes in v10:
time: 96.1 us; the launch traced here: 96 us
  Pallas kernels  95.3 us (99%)
    pallas_call x1, Pallas kernels, all_steps(): pl.pallas_call(functools.partial(kernel, lons, levs), out_shape=(inner, i...  76.1 us
    pallas_call x1, Pallas kernels, all_steps(): pl.pallas_call(functools.partial(last_row, lons), out_shape=(row, row) +...  15 us
    pallas_call x1, Pallas kernels, all_steps(): pl.pallas_call(write_inner, out_shape=(out, out, pltpu.VMEM((8, lanes), j...  3.02 us

profile of v10, /device:TPU:1, one launch (start us, length us, event | category | flops | bytes accessed | tf_op | source)
XLA Modules:
  0.0 96.0 jit_solution(4863405308651153525)
XLA Ops:
  0.6 76.1 %shard_map.41 = (f32[3,16,128,128]{3,2,1,0:T(8,128)S(1)}, f32[3,16,128,128]{3,2,1,0:T(8,128)S(1)}, f32[16,128,128]{2,1,0:T(8,128)S(1)}, f32[16,128,128]{2,1,0:T(8,128)S(1)}) custom-call(f32[4,16,128,128]{3,2,1,0:T(8,128)} %dens.1, f32[4,16,128,128]{3,2,1,0:T(8,128)} %crowd.1), custom_call_target="tpu_custom_call" | custom-call | tf_op jit(solution)/shard_map/pallas_call | solution.py:629
  76.7 3.0 %shard_map.42 = (f32[4,16,128,128]{3,2,1,0:T(8,128)}, f32[4,16,128,128]{3,2,1,0:T(8,128)}, f32[8,128]{1,0:T(8,128)S(1)}) custom-call(f32[3,16,128,128]{3,2,1,0:T(8,128)S(1)} %get-tuple-element.16.scaled, f32[3,16,128,128]{3,2,1,0:T(8,128)S(1)} %get-tuple-element.17.dens, f32[16,128,128]{2,1,0:T(8,128)S(1)} %get-tuple-element.14.edge), custom_call_target="tpu_custom_call" | custom-call | tf_op jit(solution)/shard_map/pallas_call | solution.py:656
  79.7 15.0 %shard_map.43 = (f32[16,128,128]{2,1,0:T(8,128)S(1)}, f32[16,128,128]{2,1,0:T(8,128)S(1)}, f32[16,8,128]{2,1,0:T(8,128)S(1)}, f32[16,8,128]{2,1,0:T(8,128)S(1)}, f32[2,8,128]{2,1,0:T(8,128)S(1)}) custom-call(f32[16,128,128]{2,1,0:T(8,128)S(1)} %get-tuple-element.14.edge, f32[16,128,128]{2,1,0:T(8,128)S(1)} %get-tuple-element.15.front, ...), custom_call_target="tpu_custom_call" | custom-call | tf_op jit(solution)/shard_map/pallas_call | solution.py:668
  94.7 1.3 %shard_map.44 = (f32[4,16,128,128]{3,2,1,0:T(8,128)}, f32[4,16,128,128]{3,2,1,0:T(8,128)}) custom-call(f32[16,128,128]{2,1,0:T(8,128)S(1)} %get-tuple-element.19.scaled, f32[16,128,128]{2,1,0:T(8,128)S(1)} %get-tuple-element.20.dens, f32[16,8,128]{2,1,0:T(8,128)S(1)} %get-tuple-element.21.refs_0_, ...), custom_call_target="tpu_custom_call", output_to_operand_aliasing={{0}: (5, {}), {1}: (6, {})} | custom-call | tf_op jit(solution)/shard_map/pallas_call | solution.py:692

commit v11 on v10

--- a/solution.py
+++ b/solution.py
@@ -78,7 +78,7 @@
 
 def split(deep):
     half, last = deep // 2, deep - 8
-    first, late = max(8, deep // 32 * 8), max(8, deep // 64 * 8)
+    first, late = max(8, 5 * deep // 128 * 8), max(8, deep // 64 * 8)
     coarse = [(0, half), (half, half)]
     fine = [(0, first), (first, last - late - first), (last - late, late), (last, 8)]
     return coarse, fine
@@ -461,7 +461,7 @@
         where = {"lat": 1 - lat} if i < 2 else {}
         if i > 0:
             where["lon"] = 1 - lon
-        return remote(src, dst, tile_send.at[i % 3], tile_recv.at[i // 2], where)
+        return remote(src, dst, tile_send.at[0], tile_recv.at[i // 2], where)
 
     def stat(part, j):
         pick = (slice(None), pl.ds(*spans[part]))
@@ -549,8 +549,9 @@
         @pl.when(late)
         def _():
             tile_base[...] = edge[:, tail]
-            for i in range(3):
-                tile_copy(i).wait_send()
+            pick = (slice(None), pl.ds(0, 24))
+            remote(front.at[pick], other.at[pick], tile_send.at[0], tile_recv.at[0],
+                   {"lat": 1 - lat}).wait_send()
             tile_copy(3).wait_recv()
             tile_copy(0).wait_recv()
     else:
@@ -563,7 +564,7 @@
     twin = lons == 2
     if twin:
         tile_base, tile_face, tile_sums, _, _, out_scaled, out_dens, sems = refs[:8]
-        own_scaled, own_dens, tile_sem = refs[8:]
+        own_scaled, own_dens = refs[8:]
     else:
         _, _, out_scaled, out_dens, sems = refs
     rows = out_dens.shape[0]
@@ -577,20 +578,19 @@
         return pltpu.make_async_copy(
             src.at[:, span], dst.at[place(1, rows), :, span], sems.at[i])
 
-    def each(act):
-        act(copy(scaled, out_scaled, 0, 0, last if twin else deep))
+    def each(act, stop):
+        act(copy(scaled, out_scaled, 0, 0, stop))
         for moved in range(2):
             @pl.when(late == moved)
             def _():
-                stop = last if twin and moved else deep
-                act(copy(dens, out_dens, 1, sum(fine[moved]), stop))
+                act(copy(dens, out_dens, 1, sum(fine[moved]), stop if moved else deep))
 
     def tile_out(i):
         src, dst = ((own_scaled, out_scaled), (own_dens, out_dens))[i]
         return pltpu.make_async_copy(
-            src, dst.at[place(1, rows), :, pl.ds(last, 8)], tile_sem.at[i])
-
-    each(lambda copy: copy.start())
+            src, dst.at[place(1, rows), :, pl.ds(last, 8)], sems.at[i])
+
+    each(lambda copy: copy.start(), last if twin else deep)
     if twin:
         values = [tile_base[c] + 0.1 * tile_face[c] for c in range(cols)]
         mean, gain = line_scale([line_sums(values), (tile_sums[0], tile_sums[1])], cols)
@@ -608,9 +608,7 @@
                 own_scaled[c] = (dens[c, pl.ds(last, 8)] - mean) * gain
 
         tile_out(0).start()
-        pl.when(late == 1)(lambda: tile_out(1).wait())
-        tile_out(0).wait()
-    each(lambda copy: copy.wait())
+    each(lambda copy: copy.wait(), deep)
 
 
 def in_vmem(*arrays):
@@ -679,7 +677,7 @@
             sem((len(fine) - 1,)),
             sem((peers,)),
             sem((2 if twin else 3, peers)),
-            sem((3,)),
+            sem((1,)),
             sem((2,)),
         ],
         compiler_params=pltpu.CompilerParams(
@@ -695,7 +693,7 @@
         in_specs=[vmem] * known + [hbm] * 2,
         out_specs=[hbm] * 2,
         input_output_aliases={known: 0, known + 1: 1},
-        scratch_shapes=[sem((2,))] + ([tile, tile, sem((2,))] if twin else []),
+        scratch_shapes=[sem((2,))] + ([tile, tile] if twin else []),
         compiler_params=pltpu.CompilerParams(vmem_limit_bytes=2**20),
     )(*in_vmem(*row_parts), out_scaled, out_dens)
 

time: 96.1 us -> 96.1 us (level)
    pallas_call x1, Pallas kernels: 15 us -> 13.5 us  [all_steps(): pl.pallas_call(functools.partial(last_row, lons), out_shape=(row, row) +...]
    pallas_call x1, Pallas kernels: 76.1 us -> 77.5 us  [all_steps(): pl.pallas_call(functools.partial(kernel, lons, levs), out_shape=(inner, i...]
where the time goes in v11:
time: 96.1 us; the launch traced here: 95.9 us
  Pallas kernels  95.3 us (99%)
    pallas_call x1, Pallas kernels, all_steps(): pl.pallas_call(functools.partial(kernel, lons, levs), out_shape=(inner, i...  77.5 us
    pallas_call x1, Pallas kernels, all_steps(): pl.pallas_call(functools.partial(last_row, lons), out_shape=(row, row) +...  13.5 us
    pallas_call x1, Pallas kernels, all_steps(): pl.pallas_call(write_inner, out_shape=(out, out, pltpu.VMEM((8, lanes), j...  3.02 us

profile of v11, /device:TPU:1, one launch (start us, length us, event | category | flops | bytes accessed | tf_op | source)
XLA Modules:
  0.0 95.9 jit_solution(9978513715825721603)
XLA Ops:
  0.6 77.5 %shard_map.41 = (f32[3,16,128,128]{3,2,1,0:T(8,128)S(1)}, f32[3,16,128,128]{3,2,1,0:T(8,128)S(1)}, f32[16,128,128]{2,1,0:T(8,128)S(1)}, f32[16,128,128]{2,1,0:T(8,128)S(1)}) custom-call(f32[4,16,128,128]{3,2,1,0:T(8,128)} %dens.1, f32[4,16,128,128]{3,2,1,0:T(8,128)} %crowd.1), custom_call_target="tpu_custom_call" | custom-call | tf_op jit(solution)/shard_map/pallas_call | solution.py:627
  78.1 3.0 %shard_map.42 = (f32[4,16,128,128]{3,2,1,0:T(8,128)}, f32[4,16,128,128]{3,2,1,0:T(8,128)}, f32[8,128]{1,0:T(8,128)S(1)}) custom-call(f32[3,16,128,128]{3,2,1,0:T(8,128)S(1)} %get-tuple-element.16.scaled, f32[3,16,128,128]{3,2,1,0:T(8,128)S(1)} %get-tuple-element.17.dens, f32[16,128,128]{2,1,0:T(8,128)S(1)} %get-tuple-element.14.edge), custom_call_target="tpu_custom_call" | custom-call | tf_op jit(solution)/shard_map/pallas_call | solution.py:654
  81.2 13.5 %shard_map.43 = (f32[16,128,128]{2,1,0:T(8,128)S(1)}, f32[16,128,128]{2,1,0:T(8,128)S(1)}, f32[16,8,128]{2,1,0:T(8,128)S(1)}, f32[16,8,128]{2,1,0:T(8,128)S(1)}, f32[2,8,128]{2,1,0:T(8,128)S(1)}) custom-call(f32[16,128,128]{2,1,0:T(8,128)S(1)} %get-tuple-element.14.edge, f32[16,128,128]{2,1,0:T(8,128)S(1)} %get-tuple-element.15.front, ...), custom_call_target="tpu_custom_call" | custom-call | tf_op jit(solution)/shard_map/pallas_call | solution.py:666
  94.7 1.2 %shard_map.44 = (f32[4,16,128,128]{3,2,1,0:T(8,128)}, f32[4,16,128,128]{3,2,1,0:T(8,128)}) custom-call(f32[16,128,128]{2,1,0:T(8,128)S(1)} %get-tuple-element.19.scaled, f32[16,128,128]{2,1,0:T(8,128)S(1)} %get-tuple-element.20.dens, f32[16,8,128]{2,1,0:T(8,128)S(1)} %get-tuple-element.21.refs_0_, ...), custom_call_target="tpu_custom_call", output_to_operand_aliasing={{0}: (5, {}), {1}: (6, {})} | custom-call | tf_op jit(solution)/shard_map/pallas_call | solution.py:690

commit v12 on v11

--- a/solution.py
+++ b/solution.py
@@ -386,10 +386,10 @@
         lax.fori_loop(0, cols, col, 0)
 
     wait_sides_sent()
+    pl.when(jnp.logical_not(late))(lambda: face(t - 1, 1).wait_send())
+    add_face(0)
     for j in range(1, lons):
         stat(0, j).wait_send()
-    pl.when(jnp.logical_not(late))(lambda: face(t - 1, 1).wait_send())
-    add_face(0)
     face(t, 0).wait_send()
 
     @pl.when(late)
@@ -483,7 +483,7 @@
         for k in range(2, end if twin else end + 1):
             face(k).start()
         if twin:
-            for i in (2, 0, 1):
+            for i in (0, 1, 2):
                 tile_copy(i).start()
 
     for j in range(1, lons):

time: 96.1 us -> 96.1 us (level)
  no operation moved by 1% of the time
where the time goes in v12:
time: 96.1 us; the launch traced here: 95.9 us
  Pallas kernels  95.3 us (99%)
    pallas_call x1, Pallas kernels, all_steps(): pl.pallas_call(functools.partial(kernel, lons, levs), out_shape=(inner, i...  77.5 us
    pallas_call x1, Pallas kernels, all_steps(): pl.pallas_call(functools.partial(last_row, lons), out_shape=(row, row) +...  13.5 us
    pallas_call x1, Pallas kernels, all_steps(): pl.pallas_call(write_inner, out_shape=(out, out, pltpu.VMEM((8, lanes), j...  3.02 us

profile of v12, /device:TPU:1, one launch (start us, length us, event | category | flops | bytes accessed | tf_op | source)
XLA Modules:
  0.0 95.9 jit_solution(16061240466454147344)
XLA Ops:
  0.6 77.5 %shard_map.41 = (f32[3,16,128,128]{3,2,1,0:T(8,128)S(1)}, f32[3,16,128,128]{3,2,1,0:T(8,128)S(1)}, f32[16,128,128]{2,1,0:T(8,128)S(1)}, f32[16,128,128]{2,1,0:T(8,128)S(1)}) custom-call(f32[4,16,128,128]{3,2,1,0:T(8,128)} %dens.1, f32[4,16,128,128]{3,2,1,0:T(8,128)} %crowd.1), custom_call_target="tpu_custom_call" | custom-call | tf_op jit(solution)/shard_map/pallas_call | solution.py:627
  78.1 3.0 %shard_map.42 = (f32[4,16,128,128]{3,2,1,0:T(8,128)}, f32[4,16,128,128]{3,2,1,0:T(8,128)}, f32[8,128]{1,0:T(8,128)S(1)}) custom-call(f32[3,16,128,128]{3,2,1,0:T(8,128)S(1)} %get-tuple-element.16.scaled, f32[3,16,128,128]{3,2,1,0:T(8,128)S(1)} %get-tuple-element.17.dens, f32[16,128,128]{2,1,0:T(8,128)S(1)} %get-tuple-element.14.edge), custom_call_target="tpu_custom_call" | custom-call | tf_op jit(solution)/shard_map/pallas_call | solution.py:654
  81.2 13.5 %shard_map.43 = (f32[16,128,128]{2,1,0:T(8,128)S(1)}, f32[16,128,128]{2,1,0:T(8,128)S(1)}, f32[16,8,128]{2,1,0:T(8,128)S(1)}, f32[16,8,128]{2,1,0:T(8,128)S(1)}, f32[2,8,128]{2,1,0:T(8,128)S(1)}) custom-call(f32[16,128,128]{2,1,0:T(8,128)S(1)} %get-tuple-element.14.edge, f32[16,128,128]{2,1,0:T(8,128)S(1)} %get-tuple-element.15.front, ...), custom_call_target="tpu_custom_call" | custom-call | tf_op jit(solution)/shard_map/pallas_call | solution.py:666
  94.7 1.2 %shard_map.44 = (f32[4,16,128,128]{3,2,1,0:T(8,128)}, f32[4,16,128,128]{3,2,1,0:T(8,128)}) custom-call(f32[16,128,128]{2,1,0:T(8,128)S(1)} %get-tuple-element.19.scaled, f32[16,128,128]{2,1,0:T(8,128)S(1)} %get-tuple-element.20.dens, f32[16,8,128]{2,1,0:T(8,128)S(1)} %get-tuple-element.21.refs_0_, ...), custom_call_target="tpu_custom_call", output_to_operand_aliasing={{0}: (5, {}), {1}: (6, {})} | custom-call | tf_op jit(solution)/shard_map/pallas_call | solution.py:690
